TPU v7x, 16 devices: a whole 2x2x2 slice. The times are simulated.
16 devices in a mesh: dp: 2 (over z), fsdp: 8 (over y, x, core).
Axes of the slice: x: 2, y: 2, z: 2, core: 2. Of those that a mesh axis runs over, the one named last changes fastest.
Arguments:
- hidden: bfloat16 [16, 64, 1536], P(('dp', 'fsdp')), parts along dimension 0
- attn_norm: bfloat16 [2, 1536], P(None, 'fsdp')
- w_q: bfloat16 [2, 1536, 12, 128], P(None, 'fsdp')
- w_k: bfloat16 [2, 1536, 2, 128], P(None, 'fsdp')
- w_v: bfloat16 [2, 1536, 2, 128], P(None, 'fsdp')
- w_o: bfloat16 [2, 1536, 1536], P(None, 'fsdp')
- mlp_norm: bfloat16 [2, 1536], P(None, 'fsdp')
- w_gate: bfloat16 [2, 1536, 8960], P(None, 'fsdp')
- w_up: bfloat16 [2, 1536, 8960], P(None, 'fsdp')
- w_down: bfloat16 [2, 8960, 1536], P(None, 'fsdp')
Outputs:
- output: bfloat16 [16, 64, 1536], P(('dp', 'fsdp')), parts along dimension 0
There are 2 independent parts. A program takes and returns all parts, laid end to end along the dimension named above; an argument that names none is the same for every part.
All inputs are finite; a program needn't handle non-finite values.
Results may differ from a plain program's by a relative error of at most 0.02.
Values are sent between devices in bfloat16 or wider.
A program may use at most 1 GiB of HBM per device.

v0:
```python
import jax
import jax.numpy as jnp
from jax import lax
from jax.sharding import PartitionSpec as P

ROPE_THETA = 500000.0
NORM_EPS = 1e-5


def rms_norm(hidden, gain):
    wide_hidden = hidden.astype(jnp.float32)
    inv_rms = lax.rsqrt(jnp.mean(wide_hidden * wide_hidden, axis=-1, keepdims=True) + NORM_EPS)
    return (wide_hidden * inv_rms * gain.astype(jnp.float32)).astype(jnp.bfloat16)


def rope_tables(seq_len, head_dim):
    half = head_dim // 2
    inv_freq = jnp.power(ROPE_THETA, -(jnp.arange(half, dtype=jnp.float32) * 2.0 / head_dim))
    angles = jnp.arange(seq_len, dtype=jnp.float32)[:, None] * inv_freq[None, :]
    return jnp.cos(angles)[:, None, :], jnp.sin(angles)[:, None, :]


def apply_rope(proj, cos_table, sin_table):
    half = proj.shape[-1] // 2
    first = proj[..., :half]
    second = proj[..., half:]
    rotated = jnp.concatenate([first * cos_table - second * sin_table, second * cos_table + first * sin_table], axis=-1)
    return rotated.astype(jnp.bfloat16)


def decoder_layer(hidden, attn_gain, w_q, w_k, w_v, w_o, mlp_gain, w_gate, w_up, w_down):
    batch, seq_len = hidden.shape[0], hidden.shape[1]
    heads, head_dim = w_q.shape[1], w_q.shape[2]
    kv_heads = w_k.shape[1]
    group = heads // kv_heads
    cos_table, sin_table = rope_tables(seq_len, head_dim)
    normed = rms_norm(hidden, attn_gain)
    queries = apply_rope(jnp.einsum("bsd,dhe->bshe", normed, w_q, preferred_element_type=jnp.float32), cos_table, sin_table)
    keys_rot = apply_rope(jnp.einsum("bsd,dhe->bshe", normed, w_k, preferred_element_type=jnp.float32), cos_table, sin_table)
    values = jnp.einsum("bsd,dhe->bshe", normed, w_v, preferred_element_type=jnp.float32).astype(jnp.bfloat16)
    q_grouped = queries.reshape(batch, seq_len, kv_heads, group, head_dim)
    scores = jnp.einsum("bqkgd,bskd->bkgqs", q_grouped, keys_rot, preferred_element_type=jnp.float32) * head_dim ** -0.5
    row_pos = lax.broadcasted_iota(jnp.int32, (seq_len, seq_len), 0)
    col_pos = lax.broadcasted_iota(jnp.int32, (seq_len, seq_len), 1)
    probs = jax.nn.softmax(jnp.where(row_pos >= col_pos, scores, -jnp.inf), axis=-1).astype(jnp.bfloat16)
    attended = jnp.einsum("bkgqs,bskd->bqkgd", probs, values, preferred_element_type=jnp.float32).astype(jnp.bfloat16)
    attended = attended.reshape(batch, seq_len, heads * head_dim)
    after_attn = (hidden.astype(jnp.float32) + jnp.einsum("bsf,fd->bsd", attended, w_o, preferred_element_type=jnp.float32)).astype(jnp.bfloat16)
    mlp_in = rms_norm(after_attn, mlp_gain)
    gate_proj = jnp.einsum("bsd,df->bsf", mlp_in, w_gate, preferred_element_type=jnp.float32).astype(jnp.bfloat16)
    up_proj = jnp.einsum("bsd,df->bsf", mlp_in, w_up, preferred_element_type=jnp.float32).astype(jnp.bfloat16)
    gated = (jax.nn.silu(gate_proj.astype(jnp.float32)) * up_proj.astype(jnp.float32)).astype(jnp.bfloat16)
    return (after_attn.astype(jnp.float32) + jnp.einsum("bsf,fd->bsd", gated, w_down, preferred_element_type=jnp.float32)).astype(jnp.bfloat16)


def solution(mesh):
    batch_spec = P(("dp", "fsdp"), None, None)
    gain_spec = P(None, "fsdp")
    proj_spec = P(None, "fsdp", None, None)
    mat_spec = P(None, "fsdp", None)

    def local_forward(hidden, attn_norm, w_q, w_k, w_v, w_o, mlp_norm, w_gate, w_up, w_down):
        for layer in range(w_q.shape[0]):
            whole = [lax.all_gather(shard[layer], "fsdp", axis=0, tiled=True) for shard in (attn_norm, w_q, w_k, w_v, w_o, mlp_norm, w_gate, w_up, w_down)]
            hidden = decoder_layer(hidden, whole[0], whole[1], whole[2], whole[3], whole[4], whole[5], whole[6], whole[7], whole[8])
        return hidden

    return jax.shard_map(local_forward, mesh=mesh, in_specs=(batch_spec, gain_spec, proj_spec, proj_spec, proj_spec, mat_spec, gain_spec, mat_spec, mat_spec, mat_spec), out_specs=batch_spec, check_vma=False)
```

profile of v0, /device:TPU:0, one launch (start us, length us, event | category | flops | bytes accessed | tf_op | source)
XLA Modules:
  0.0 990.9 jit_solution(10309767229225997577)
XLA Ops:
  6.5 2.5 fusion.188
  9.1 1.1 fusion.187
  10.2 6.3 fusion.184
  16.6 6.2 fusion.185
  22.9 6.2 fusion.186
  29.8 0.7 all-gather.41.cloned.1.call-update
  30.6 0.7 all-gather.43.cloned.1.call-update
  31.4 0.6 all-gather.45.cloned.1.call-update
  32.6 0.6 dynamic-slice
  34.9 26.1 %all-reduce.4 = (bf16[1536]{0:T(1024)(128)(2,1)S(1)}, bf16[1536]{0:T(1024)(128)(2,1)S(1)}, bf16[1536]{0:T(1024)(128)(2,1)S(1)}, bf16[1536]{0:T(1024)(128)(2,1)S(1)}) all-reduce(bf16[1536]{0:T(1024)(128)(2,1)S(1)} %dynamic-update-slice, bf16[1536]{0:T(1024)(128)(2,1)S(1)} %dynamic-update-slice.1, ...), channel_id=2, replica_groups=mesh['dp'=2,'fsdp'=8] {'fsdp'}, use_global_device_ids=true, to_apply=%add | all-reduce | flops 6144 | bytes 24576
  61.4 9.7 all-gather.2
  71.5 15.2 %all-gather.1 = bf16[1,1536,2,128]{3,2,0,1:T(2,128)(2,1)S(1)} all-gather(bf16[1,192,2,128]{3,2,0,1:T(2,128)(2,1)S(1)} %get-tuple-element.30), channel_id=3, replica_groups=mesh['dp'=2,'fsdp'=8] {'fsdp'}, dimensions={1}, use_global_device_ids=true | all-gather | bytes 884736 | tf_op jit(solution)/shard_map/all_gather | solution.py:64
  86.7 10.2 %all-gather.11 = bf16[1,1536,2,128]{3,1,2,0:T(8,128)(2,1)} all-gather(bf16[1,192,2,128]{3,1,2,0:T(8,128)(2,1)S(1)} %copy.40), channel_id=13, replica_groups=mesh['dp'=2,'fsdp'=8] {'fsdp'}, dimensions={1}, use_global_device_ids=true | all-gather | bytes 884736 | tf_op jit(solution)/shard_map/all_gather | solution.py:64
  96.9 14.0 %all-gather.10 = bf16[1,1536,2,128]{3,2,0,1:T(2,128)(2,1)} all-gather(bf16[1,192,2,128]{3,2,0,1:T(2,128)(2,1)S(1)} %get-tuple-element.29), channel_id=12, replica_groups=mesh['dp'=2,'fsdp'=8] {'fsdp'}, dimensions={1}, use_global_device_ids=true | all-gather | bytes 884736 | tf_op jit(solution)/shard_map/all_gather | solution.py:64
  111.2 3.3 fusion.103
  115.2 0.6 fusion.111
  116.2 3.4 multiply_reduce_fusion.2
  119.6 104.1 %all-gather.33.cloned.1.call-done = bf16[1,1536,8960]{2,1,0:T(8,128)(2,1)} async-done(((bf16[1,192,8960]{2,1,0:T(8,128)(2,1)}), bf16[1,1536,8960]{2,1,0:T(8,128)(2,1)}) %all-gather.33.cloned.1.call-update) | async-done | bytes 27525136 | tf_op jit(solution)/shard_map/all_gather | solution.py:64
  223.7 11.4 %fusion.15 = f32[64,8960]{1,0:T(8,128)S(1)} fusion(bf16[1,1536,8960]{2,1,0:T(8,128)(2,1)} %all-gather.33.cloned.1.call-done, f32[1,64,1536]{2,1,0:T(8,128)S(1)} %get-tuple-element.40, f32[1536]{0:T(1024)S(1)} %convert_element_type.183, f32[64]{0:T(128)S(1)} %add_rsqrt_fusion.2), kind=kOutput, calls=%fused_computation.13 | convolution fusion | flops 1763049472 | bytes 30218496 | tf_op jit(solution)/shard_map/bsd,df->bsf/dot_general | solution.py:50
  235.1 121.8 %all-gather.35.cloned.1.call-done = bf16[1,1536,8960]{2,1,0:T(8,128)(2,1)} async-done(((bf16[1,192,8960]{2,1,0:T(8,128)(2,1)}), bf16[1,1536,8960]{2,1,0:T(8,128)(2,1)}) %all-gather.35.cloned.1.call-update) | async-done | bytes 27525136 | tf_op jit(solution)/shard_map/all_gather | solution.py:64
  356.9 133.2 %all-gather.37.cloned.1.call-done = bf16[1,8960,1536]{2,1,0:T(8,128)(2,1)} async-done(((bf16[1,1120,1536]{2,1,0:T(8,128)(2,1)}), bf16[1,8960,1536]{2,1,0:T(8,128)(2,1)}) %all-gather.37.cloned.1.call-update) | async-done | bytes 27525136 | tf_op jit(solution)/shard_map/all_gather | solution.py:64
  490.1 20.5 %multiply_reduce_fusion.1 = (f32[64]{0:T(128)S(1)}, f32[1,64,1536]{2,1,0:T(8,128)S(1)}) fusion(f32[1,64,1536]{2,1,0:T(8,128)S(1)} %get-tuple-element.40, bf16[1,8960,1536]{2,1,0:T(8,128)(2,1)} %all-gather.37.cloned.1.call-done, bf16[1,1536,8960]{2,1,0:T(8,128)(2,1)} %all-gather.35.cloned.1.call-done, f32[64,8960]{1,0:T(8,128)S(1)} %fusion.15, ...), kind=kOutput, calls=%fused_computation.83 | convolution fusion | flops 3528589312 | bytes 58137088 | tf_op jit(solution)/shard_map/bsf,fd->bsd/dot_general | solution.py:53
  510.7 1.4 convolution_bitcast_fusion
  512.2 14.4 %all-gather.39.cloned.1.call-done = bf16[1,1536,12,128]{3,1,2,0:T(8,128)(2,1)} async-done(((bf16[1,192,12,128]{3,1,2,0:T(8,128)(2,1)}), bf16[1,1536,12,128]{3,1,2,0:T(8,128)(2,1)}) %all-gather.39.cloned.1.call-update) | async-done | bytes 4718608 | tf_op jit(solution)/shard_map/all_gather | solution.py:64
  526.6 3.3 fusion.106
  531.5 31.7 %all-gather.41.cloned.1.call-done = bf16[1,1536,1536]{2,1,0:T(8,128)(2,1)} async-done(((bf16[1,192,1536]{2,1,0:T(8,128)(2,1)}), bf16[1,1536,1536]{2,1,0:T(8,128)(2,1)}) %all-gather.41.cloned.1.call-update) | async-done | bytes 4718608 | tf_op jit(solution)/shard_map/all_gather | solution.py:64
  563.2 3.4 multiply_reduce_fusion
  566.6 129.9 %all-gather.43.cloned.1.call-done = bf16[1,1536,8960]{2,1,0:T(8,128)(2,1)} async-done(((bf16[1,192,8960]{2,1,0:T(8,128)(2,1)}), bf16[1,1536,8960]{2,1,0:T(8,128)(2,1)}) %all-gather.43.cloned.1.call-update) | async-done | bytes 27525136 | tf_op jit(solution)/shard_map/all_gather | solution.py:64
  696.5 11.4 %fusion.33 = f32[64,8960]{1,0:T(8,128)S(1)} fusion(bf16[1,1536,8960]{2,1,0:T(8,128)(2,1)} %all-gather.43.cloned.1.call-done, f32[1,64,1536]{2,1,0:T(8,128)S(1)} %get-tuple-element.46, f32[1536]{0:T(1024)S(1)} %convert_element_type.185, f32[64]{0:T(128)S(1)} %add_rsqrt_fusion), kind=kOutput, calls=%fused_computation.19 | convolution fusion | flops 1763049472 | bytes 30218496 | tf_op jit(solution)/shard_map/bsd,df->bsf/dot_general | solution.py:50
  707.9 122.0 %all-gather.45.cloned.1.call-done = bf16[1,1536,8960]{2,1,0:T(8,128)(2,1)} async-done(((bf16[1,192,8960]{2,1,0:T(8,128)(2,1)}), bf16[1,1536,8960]{2,1,0:T(8,128)(2,1)}) %all-gather.45.cloned.1.call-update) | async-done | bytes 27525136 | tf_op jit(solution)/shard_map/all_gather | solution.py:64
  829.9 133.2 %all-gather.47.cloned.1.call-done = bf16[1,8960,1536]{2,1,0:T(8,128)(2,1)} async-done(((bf16[1,1120,1536]{2,1,0:T(8,128)(2,1)}), bf16[1,8960,1536]{2,1,0:T(8,128)(2,1)}) %all-gather.47.cloned.1.call-update) | async-done | bytes 27525136 | tf_op jit(solution)/shard_map/all_gather | solution.py:64
  963.0 21.0 %fusion.86 = bf16[1,64,1536]{2,1,0:T(8,128)(2,1)} fusion(f32[1,64,1536]{2,1,0:T(8,128)S(1)} %get-tuple-element.46, bf16[1,8960,1536]{2,1,0:T(8,128)(2,1)} %all-gather.47.cloned.1.call-done, bf16[1,1536,8960]{2,1,0:T(8,128)(2,1)} %all-gather.45.cloned.1.call-done, f32[64,8960]{1,0:T(8,128)S(1)} %fusion.33, f32[1536]{0:T(1024)S(1)} %convert_element_type.185, ...), kind=kOutput, calls=%fused_computation.42 | convolution fusion | flops 3528294400 | bytes 57940224 | tf_op jit(solution)/shard_map/bsf,fd->bsd/dot_general | solution.py:53
  (76 shorter events, 6.5 us)
Async XLA Ops:
  6.5 2.5 copy-start.1
  6.5 104.7 %all-gather.29.cloned.1.call-start = ((), (), s32[]{:S(2)}) async-start(), calls=%async_computation | async-start | bytes 5308416 | tf_op jit(solution)/shard_map/all_gather | solution.py:64
  9.0 107.2 %all-gather.31.cloned.1.call-start = ((), (), s32[]{:S(2)}) async-start(), calls=%async_computation.1 | async-start | bytes 5308416 | tf_op jit(solution)/shard_map/all_gather | solution.py:64
  10.2 213.5 %all-gather.33.cloned.1.call-start = ((), (), s32[]{:S(2)}) async-start(), calls=%async_computation.2 | async-start | bytes 30965760 | tf_op jit(solution)/shard_map/all_gather | solution.py:64
  16.6 340.3 %all-gather.35.cloned.1.call-start = ((), (), s32[]{:S(2)}) async-start(), calls=%async_computation.3 | async-start | bytes 30965760 | tf_op jit(solution)/shard_map/all_gather | solution.py:64
  22.9 467.2 %all-gather.37.cloned.1.call-start = ((), (), s32[]{:S(2)}) async-start(), calls=%async_computation.4 | async-start | bytes 30965760 | tf_op jit(solution)/shard_map/all_gather | solution.py:64
  29.2 497.4 %all-gather.39.cloned.1.call-start = ((), (), s32[]{:S(2)}) async-start(), calls=%async_computation.5 | async-start | bytes 5308416 | tf_op jit(solution)/shard_map/all_gather | solution.py:64
  29.8 533.4 %all-gather.41.cloned.1.call-start = ((), (), s32[]{:S(2)}) async-start(), calls=%async_computation.6 | async-start | bytes 5308416 | tf_op jit(solution)/shard_map/all_gather | solution.py:64
  30.5 666.0 %all-gather.43.cloned.1.call-start = ((), (), s32[]{:S(2)}) async-start(), calls=%async_computation.7 | async-start | bytes 30965760 | tf_op jit(solution)/shard_map/all_gather | solution.py:64
  31.3 798.6 %all-gather.45.cloned.1.call-start = ((), (), s32[]{:S(2)}) async-start(), calls=%async_computation.8 | async-start | bytes 30965760 | tf_op jit(solution)/shard_map/all_gather | solution.py:64
  31.3 1.3 copy-start.7
  31.3 2.5 copy-start.5
  31.3 2.8 copy-start.6
  31.3 29.7 %copy-start.3 = (bf16[2,192,2,128]{3,2,1,0:T(2,128)(2,1)S(1)}, bf16[2,192,2,128]{3,2,1,0:T(2,128)(2,1)}, u32[]{:S(2)}) copy-start(bf16[2,192,2,128]{3,2,1,0:T(2,128)(2,1)} %param.13) | copy-start | bytes 589828
  31.4 29.9 %copy-start = (bf16[1,64,1536]{2,1,0:T(8,128)(2,1)S(1)}, bf16[1,64,1536]{2,1,0:T(8,128)(2,1)}, u32[]{:S(2)}) copy-start(bf16[1,64,1536]{2,1,0:T(8,128)(2,1)} %param.10) | copy-start | bytes 589828
  32.0 39.4 %copy-start.4 = (bf16[2,192,2,128]{3,2,1,0:T(2,128)(2,1)S(1)}, bf16[2,192,2,128]{3,2,1,0:T(2,128)(2,1)}, u32[]{:S(2)}) copy-start(bf16[2,192,2,128]{3,2,1,0:T(2,128)(2,1)} %param.14) | copy-start | bytes 589828
  32.0 931.0 %all-gather.47.cloned.1.call-start = ((), (), s32[]{:S(2)}) async-start(), calls=%async_computation.9 | async-start | bytes 30965760 | tf_op jit(solution)/shard_map/all_gather | solution.py:64
  512.2 18.4 %copy-start.2 = (bf16[1,1536,2,128]{3,2,0,1:T(2,128)(2,1)S(1)}, bf16[1,1536,2,128]{3,2,0,1:T(2,128)(2,1)}, u32[]{:S(2)}) copy-start(bf16[1,1536,2,128]{3,2,0,1:T(2,128)(2,1)} %all-gather.10) | copy-start | bytes 2359300
Sparse Core Ops, SparseCore 0:
  9.2 37.6 all-gather.28
  48.7 38.2 all-gather.30
  88.9 134.7 all-gather.32
  225.4 131.4 all-gather.34
  358.6 131.4 all-gather.36
  491.8 34.7 all-gather.38
  528.4 34.7 all-gather.40
  565.0 131.4 all-gather.42
  698.4 131.4 all-gather.44
  831.6 131.4 all-gather.46
where the time goes:
time: 991 us
  waiting for transfers between devices  793 us (80%)
  matrix products  81.2 us (8%)
  blocking collectives  75.2 us (8%)
  local copies, waits for them, and re-layouts  25 us (3%)
  between operations  14.6 us (1%)
    all_gather x10, waiting for transfers between devices, local_forward(): lax.all_gather(shard[layer], 'fsdp', axis=0, tiled=True)  790 us
    all_gather x4, blocking collectives, local_forward(): lax.all_gather(shard[layer], 'fsdp', axis=0, tiled=True)  49 us
    dot_general x2, matrix products, decoder_layer(): jnp.einsum('bsf,fd->bsd', gated, w_down, preferred_element_type=jnp.float32)  41.5 us
    unnamed x1, blocking collectives  26.1 us
    dot_general x2, matrix products, decoder_layer(): jnp.einsum('bsd,df->bsf', mlp_in, w_gate, preferred_element_type=jnp.floa...  22.8 us
    slice x8, local copies, waits for them, and re-layouts, local_forward(): shard[layer]  22.5 us
  transfers between devices with their start and end apart: 10, of which 8 were waited for; matrix products, arithmetic and copies ran while one was open for 8% of the time, Pallas kernels for 0%

commit v1 on v0

--- a/solution.py
+++ b/solution.py
@@ -29,7 +29,7 @@
 
 
 def decoder_layer(hidden, attn_gain, w_q, w_k, w_v, w_o, mlp_gain, w_gate, w_up, w_down):
-    batch, seq_len = hidden.shape[0], hidden.shape[1]
+    batch, seq_len, width = hidden.shape
     heads, head_dim = w_q.shape[1], w_q.shape[2]
     kv_heads = w_k.shape[1]
     group = heads // kv_heads
@@ -46,11 +46,13 @@
     attended = jnp.einsum("bkgqs,bskd->bqkgd", probs, values, preferred_element_type=jnp.float32).astype(jnp.bfloat16)
     attended = attended.reshape(batch, seq_len, heads * head_dim)
     after_attn = (hidden.astype(jnp.float32) + jnp.einsum("bsf,fd->bsd", attended, w_o, preferred_element_type=jnp.float32)).astype(jnp.bfloat16)
-    mlp_in = rms_norm(after_attn, mlp_gain)
-    gate_proj = jnp.einsum("bsd,df->bsf", mlp_in, w_gate, preferred_element_type=jnp.float32).astype(jnp.bfloat16)
-    up_proj = jnp.einsum("bsd,df->bsf", mlp_in, w_up, preferred_element_type=jnp.float32).astype(jnp.bfloat16)
+    mlp_in = lax.all_gather(rms_norm(after_attn, mlp_gain).reshape(batch * seq_len, width), "fsdp", axis=0, tiled=True)
+    gate_proj = jnp.dot(mlp_in, w_gate, preferred_element_type=jnp.float32).astype(jnp.bfloat16)
+    up_proj = jnp.dot(mlp_in, w_up, preferred_element_type=jnp.float32).astype(jnp.bfloat16)
     gated = (jax.nn.silu(gate_proj.astype(jnp.float32)) * up_proj.astype(jnp.float32)).astype(jnp.bfloat16)
-    return (after_attn.astype(jnp.float32) + jnp.einsum("bsf,fd->bsd", gated, w_down, preferred_element_type=jnp.float32)).astype(jnp.bfloat16)
+    partial = jnp.dot(gated, w_down, preferred_element_type=jnp.float32)
+    down = lax.psum_scatter(partial, "fsdp", scatter_dimension=0, tiled=True).reshape(batch, seq_len, width)
+    return (after_attn.astype(jnp.float32) + down).astype(jnp.bfloat16)
 
 
 def solution(mesh):
@@ -58,11 +60,17 @@
     gain_spec = P(None, "fsdp")
     proj_spec = P(None, "fsdp", None, None)
     mat_spec = P(None, "fsdp", None)
+    size = mesh.shape["fsdp"]
+
+    def columns(shard):
+        rows, cols = shard.shape
+        blocks = shard.reshape(rows, size, cols // size).transpose(1, 0, 2)
+        return lax.all_to_all(blocks, "fsdp", 0, 0, tiled=True).reshape(rows * size, cols // size)
 
     def local_forward(hidden, attn_norm, w_q, w_k, w_v, w_o, mlp_norm, w_gate, w_up, w_down):
         for layer in range(w_q.shape[0]):
-            whole = [lax.all_gather(shard[layer], "fsdp", axis=0, tiled=True) for shard in (attn_norm, w_q, w_k, w_v, w_o, mlp_norm, w_gate, w_up, w_down)]
-            hidden = decoder_layer(hidden, whole[0], whole[1], whole[2], whole[3], whole[4], whole[5], whole[6], whole[7], whole[8])
+            whole = [lax.all_gather(shard[layer], "fsdp", axis=0, tiled=True) for shard in (attn_norm, w_q, w_k, w_v, w_o, mlp_norm)]
+            hidden = decoder_layer(hidden, *whole, columns(w_gate[layer]), columns(w_up[layer]), w_down[layer])
         return hidden
 
     return jax.shard_map(local_forward, mesh=mesh, in_specs=(batch_spec, gain_spec, proj_spec, proj_spec, proj_spec, mat_spec, gain_spec, mat_spec, mat_spec, mat_spec), out_specs=batch_spec, check_vma=False)

time: 991 us -> 471 us (0.48)
  waiting for transfers between devices: 793 us -> 164 us
  blocking collectives: 75.2 us -> 161 us
  local copies, waits for them, and re-layouts: 25 us -> 60.4 us
  matrix products: 81.2 us -> 45.9 us
  starting transfers between devices: 0.36 us -> 18 us
    all_gather x10 -> x4, waiting for transfers between devices: 790 us -> 47.4 us  [local_forward(): lax.all_gather(shard[layer], 'fsdp', axis=0, tiled=True)]
    all_to_all x0 -> x4, waiting for transfers between devices: none -> 61.7 us  [columns(): lax.all_to_all(blocks, 'fsdp', 0, 0, tiled=True)]
    all_gather x4, blocking collectives: 49 us -> 94 us  [local_forward(): lax.all_gather(shard[layer], 'fsdp', axis=0, tiled=True)]
    unnamed x1, blocking collectives: 26.1 us -> 67.1 us
    reduce_scatter x0 -> x2, waiting for transfers between devices: none -> 39.5 us  [decoder_layer(): lax.psum_scatter(partial, 'fsdp', scatter_dimension=0, tiled=True)]
    another operation x2 -> x10, local copies, waits for them, and re-layouts: 0.46 us -> 39.4 us  [the longest x8 38.9 us: columns(): blocks = shard.reshape(rows, size, cols // size).transpose(1, 0, 2)]
    dot_general x4, matrix products: 64.3 us -> 30 us  [the longest x2 18.3 us: decoder_layer(): partial = jnp.dot(gated, w_down, preferred_element_type=jnp.float32)]
    slice x8 -> x5, local copies, waits for them, and re-layouts: 22.5 us -> 4.34 us  [local_forward(): shard[layer]]
  transfers between devices with their start and end apart: 10 -> 12, of which waited for: 8 -> 7; matrix products, arithmetic and copies ran while one was open for 8% -> 19% of each run, Pallas kernels for 0% -> 0%
where the time goes in v1:
time: 471 us; the launch traced here: 470 us
  waiting for transfers between devices  164 us (35%)
  blocking collectives  161 us (34%)
  local copies, waits for them, and re-layouts  60.4 us (13%)
  matrix products  45.9 us (10%)
  starting transfers between devices  18 us (4%)
  between operations  14.6 us (3%)
  other arithmetic  5.63 us (1%)
    all_gather x4, blocking collectives, local_forward(): lax.all_gather(shard[layer], 'fsdp', axis=0, tiled=True)  94 us
    unnamed x1, blocking collectives  67.1 us
    all_to_all x4, waiting for transfers between devices, columns(): lax.all_to_all(blocks, 'fsdp', 0, 0, tiled=True)  61.7 us
    all_gather x4, waiting for transfers between devices, local_forward(): lax.all_gather(shard[layer], 'fsdp', axis=0, tiled=True)  47.4 us
    reduce_scatter x2, waiting for transfers between devices, decoder_layer(): lax.psum_scatter(partial, 'fsdp', scatter_dimension=0, tiled=True)  39.5 us
    another operation x8, local copies, waits for them, and re-layouts, columns(): blocks = shard.reshape(rows, size, cols // size).transpose(1, 0, 2)  38.9 us
    dot_general x2, matrix products, decoder_layer(): partial = jnp.dot(gated, w_down, preferred_element_type=jnp.float32)  18.3 us
    all_to_all x4, starting transfers between devices, columns(): lax.all_to_all(blocks, 'fsdp', 0, 0, tiled=True)  17.6 us
  transfers between devices with their start and end apart: 12, of which 7 were waited for; matrix products, arithmetic and copies ran while one was open for 19% of the time, Pallas kernels for 0%

profile of v1, /device:TPU:0, one launch (start us, length us, event | category | flops | bytes accessed | tf_op | source)
XLA Modules:
  0.0 469.7 jit_solution(4339429380193811221)
XLA Ops:
  6.5 2.4 fusion.126
  10.2 6.3 %fusion.123 = (bf16[1,192,8960]{2,1,0:T(8,128)(2,1)}, bf16[1,192,8960]{2,1,0:T(8,128)(2,1)}) fusion(bf16[2,192,8960]{2,1,0:T(8,128)(2,1)} %param.17), kind=kLoop, calls=%fused_computation.139 | loop fusion | bytes 13762560 | tf_op jit(solution)/shard_map/slice | solution.py:73
  16.5 7.4 %reshape_squeeze.12 = bf16[192,8,1120]{2,1,0:T(8,128)(2,1)S(1)} reshape(bf16[1,192,8960]{2,1,0:T(8,128)(2,1)} %get-tuple-element.16) | data formatting | bytes 6881280 | tf_op jit(solution)/shard_map/reshape;squeeze | solution.py:67
  26.3 5.6 %all-to-all-start = ((bf16[8,192,1120]{2,1,0:T(8,128)(2,1)}), bf16[8,192,1120]{2,1,0:T(8,128)(2,1)}, u32[]{:S(2)}, u32[]{:S(2)}) async-start(bf16[8,192,1120]{2,1,0:T(8,128)(2,1)} %bitcast.209), calls=%async_computation | async-start | bytes 7077888 | tf_op jit(solution)/shard_map/all_to_all | solution.py:68
  34.2 67.1 %all-reduce.4 = (bf16[1536]{0:T(1024)(128)(2,1)S(1)}, bf16[1536]{0:T(1024)(128)(2,1)S(1)}, bf16[1536]{0:T(1024)(128)(2,1)S(1)}, bf16[1536]{0:T(1024)(128)(2,1)S(1)}) all-reduce(bf16[1536]{0:T(1024)(128)(2,1)S(1)} %dynamic-update-slice, bf16[1536]{0:T(1024)(128)(2,1)S(1)} %dynamic-update-slice.1, ...), channel_id=2, replica_groups=mesh['dp'=2,'fsdp'=8] {'fsdp'}, use_global_device_ids=true, to_apply=%add | all-reduce | flops 6144 | bytes 24576
  102.2 12.8 %all-gather.2 = bf16[1,1536,2,128]{3,1,2,0:T(8,128)(2,1)S(1)} all-gather(bf16[1,192,2,128]{3,1,2,0:T(8,128)(2,1)S(1)} %copy.46), channel_id=4, replica_groups=mesh['dp'=2,'fsdp'=8] {'fsdp'}, dimensions={1}, use_global_device_ids=true | all-gather | bytes 884736 | tf_op jit(solution)/shard_map/all_gather | solution.py:72
  116.1 10.3 %all-gather.1 = bf16[1,1536,2,128]{3,2,0,1:T(2,128)(2,1)S(1)} all-gather(bf16[1,192,2,128]{3,2,0,1:T(2,128)(2,1)S(1)} %get-tuple-element.29), channel_id=3, replica_groups=mesh['dp'=2,'fsdp'=8] {'fsdp'}, dimensions={1}, use_global_device_ids=true | all-gather | bytes 884736 | tf_op jit(solution)/shard_map/all_gather | solution.py:72
  126.7 3.3 fusion.52
  131.7 3.4 multiply_reduce_fusion.1
  136.6 6.3 %fusion.124 = (bf16[1,192,8960]{2,1,0:T(8,128)(2,1)}, bf16[1,192,8960]{2,1,0:T(8,128)(2,1)}) fusion(bf16[2,192,8960]{2,1,0:T(8,128)(2,1)} %param.18), kind=kLoop, calls=%fused_computation.140 | loop fusion | bytes 13762560 | tf_op jit(solution)/shard_map/slice | solution.py:73
  142.9 7.4 %reshape_squeeze.13 = bf16[192,8,1120]{2,1,0:T(8,128)(2,1)S(1)} reshape(bf16[1,192,8960]{2,1,0:T(8,128)(2,1)} %get-tuple-element.18) | data formatting | bytes 6881280 | tf_op jit(solution)/shard_map/reshape;squeeze | solution.py:67
  150.3 2.3 copy.67
  152.7 3.7 all-to-all-start.1
  158.4 5.8 %fusion.19 = f32[512,1120]{0,1:T(8,128)} fusion(bf16[1536,1120]{1,0:T(8,128)(2,1)} %bitcast.25, bf16[1,512,1536]{2,1,0:T(8,128)(2,1)} %all-gather.25.cloned.1.call-done), kind=kOutput, calls=%fused_computation.27 | convolution fusion | flops 1762754560 | bytes 7307264 | tf_op jit(solution)/shard_map/dot_general | solution.py:50
  164.2 34.1 %all-to-all-done.1 = bf16[8,192,1120]{2,1,0:T(8,128)(2,1)S(1)} async-done(((bf16[8,192,1120]{2,1,0:T(8,128)(2,1)}), bf16[8,192,1120]{2,1,0:T(8,128)(2,1)S(1)}, u32[]{:S(2)}, u32[]{:S(2)}) %all-to-all-start.1) | async-done | bytes 3440672 | tf_op jit(solution)/shard_map/all_to_all | solution.py:68
  198.3 9.2 %fusion.10 = f32[512,1536]{1,0:T(8,128)} fusion(bf16[2,1120,1536]{2,1,0:T(8,128)(2,1)} %param.19, bf16[1536,1120]{1,0:T(8,128)(2,1)S(1)} %bitcast.210, f32[512,1120]{0,1:T(8,128)} %fusion.19, bf16[1,512,1536]{2,1,0:T(8,128)(2,1)} %all-gather.25.cloned.1.call-done), kind=kOutput, calls=%fused_computation.14 | convolution fusion | flops 3527802880 | bytes 13893632 | tf_op jit(solution)/shard_map/dot_general | solution.py:53
  208.7 7.4 %reshape_squeeze.14 = bf16[192,8,1120]{2,1,0:T(8,128)(2,1)S(1)} reshape(bf16[1,192,8960]{2,1,0:T(8,128)(2,1)} %get-tuple-element.15) | data formatting | bytes 6881280 | tf_op jit(solution)/shard_map/reshape;squeeze | solution.py:67
  218.4 4.6 all-to-all-start.2
  223.2 59.4 %all-gather.9 = bf16[1,1536,2,128]{3,1,2,0:T(8,128)(2,1)S(1)} all-gather(bf16[1,192,2,128]{3,1,2,0:T(8,128)(2,1)S(1)} %copy.48), channel_id=11, replica_groups=mesh['dp'=2,'fsdp'=8] {'fsdp'}, dimensions={1}, use_global_device_ids=true | all-gather | bytes 884736 | tf_op jit(solution)/shard_map/all_gather | solution.py:72
  282.6 11.6 %all-gather.8 = bf16[1,1536,2,128]{3,2,0,1:T(2,128)(2,1)S(1)} all-gather(bf16[1,192,2,128]{3,2,0,1:T(2,128)(2,1)S(1)} %copy-done.9), channel_id=10, replica_groups=mesh['dp'=2,'fsdp'=8] {'fsdp'}, dimensions={1}, use_global_device_ids=true | all-gather | bytes 884736 | tf_op jit(solution)/shard_map/all_gather | solution.py:72
  295.8 15.8 %all-gather.27.cloned.1.call-done = bf16[1,1536,12,128]{3,1,2,0:T(8,128)(2,1)} async-done(((bf16[1,192,12,128]{3,1,2,0:T(8,128)(2,1)}), bf16[1,1536,12,128]{3,1,2,0:T(8,128)(2,1)}) %all-gather.27.cloned.1.call-update) | async-done | bytes 4718608 | tf_op jit(solution)/shard_map/all_gather | solution.py:72
  311.6 3.3 fusion.55
  316.6 31.5 %all-gather.29.cloned.1.call-done = bf16[1,1536,1536]{2,1,0:T(8,128)(2,1)} async-done(((bf16[1,192,1536]{2,1,0:T(8,128)(2,1)}), bf16[1,1536,1536]{2,1,0:T(8,128)(2,1)}) %all-gather.29.cloned.1.call-update) | async-done | bytes 4718608 | tf_op jit(solution)/shard_map/all_gather | solution.py:72
  348.1 3.4 multiply_reduce_fusion
  353.1 7.4 %reshape_squeeze.15 = bf16[192,8,1120]{2,1,0:T(8,128)(2,1)S(1)} reshape(bf16[1,192,8960]{2,1,0:T(8,128)(2,1)} %get-tuple-element.17) | data formatting | bytes 6881280 | tf_op jit(solution)/shard_map/reshape;squeeze | solution.py:67
  360.5 2.3 copy.65
  362.8 3.7 all-to-all-start.3
  366.5 12.5 %all-gather.31.cloned.1.call-done = bf16[1,512,1536]{2,1,0:T(8,128)(2,1)} async-done(((bf16[1,64,1536]{2,1,0:T(8,128)(2,1)}), bf16[1,512,1536]{2,1,0:T(8,128)(2,1)}) %all-gather.31.cloned.1.call-update) | async-done | bytes 1572880 | tf_op jit(solution)/shard_map/all_gather | solution.py:49
  379.0 5.9 %fusion.16 = f32[512,1120]{0,1:T(8,128)} fusion(bf16[1536,1120]{1,0:T(8,128)(2,1)} %bitcast.54, bf16[1,512,1536]{2,1,0:T(8,128)(2,1)} %all-gather.31.cloned.1.call-done), kind=kOutput, calls=%fused_computation.22 | convolution fusion | flops 1762754560 | bytes 7307264 | tf_op jit(solution)/shard_map/dot_general | solution.py:50
  384.9 27.5 %all-to-all-done.3 = bf16[8,192,1120]{2,1,0:T(8,128)(2,1)S(1)} async-done(((bf16[8,192,1120]{2,1,0:T(8,128)(2,1)}), bf16[8,192,1120]{2,1,0:T(8,128)(2,1)S(1)}, u32[]{:S(2)}, u32[]{:S(2)}) %all-to-all-start.3) | async-done | bytes 3440672 | tf_op jit(solution)/shard_map/all_to_all | solution.py:68
  412.4 9.1 %fusion.8 = f32[512,1536]{1,0:T(8,128)} fusion(bf16[2,1120,1536]{2,1,0:T(8,128)(2,1)} %param.19, bf16[1536,1120]{1,0:T(8,128)(2,1)S(1)} %bitcast.211, f32[512,1120]{0,1:T(8,128)} %fusion.16, bf16[1,512,1536]{2,1,0:T(8,128)(2,1)} %all-gather.31.cloned.1.call-done), kind=kOutput, calls=%fused_computation.12 | convolution fusion | flops 3527802880 | bytes 13893632 | tf_op jit(solution)/shard_map/dot_general | solution.py:53
  421.6 39.5 %reduce-scatter.5.cloned.1.call-done = f32[64,1536]{1,0:T(8,128)} async-done(((f32[512,1536]{1,0:T(8,128)}), f32[64,1536]{1,0:T(8,128)}) %reduce-scatter.5.cloned.1.call-update) | async-done | bytes 393232 | tf_op jit(solution)/shard_map/reduce_scatter | solution.py:54
  (104 shorter events, 22.8 us)
Async XLA Ops:
  6.5 2.5 copy-start.4
  6.5 120.1 %all-gather.21.cloned.1.call-start = ((), (), s32[]{:S(2)}) async-start(), calls=%async_computation.8 | async-start | bytes 5308416 | tf_op jit(solution)/shard_map/all_gather | solution.py:72
  9.0 122.7 %all-gather.23.cloned.1.call-start = ((), (), s32[]{:S(2)}) async-start(), calls=%async_computation.9 | async-start | bytes 5308416 | tf_op jit(solution)/shard_map/all_gather | solution.py:72
  26.2 5.7 %copy-start.15 = (u32[16]{0:T(128)S(1)}, u32[16]{0:T(128)}, u32[]{:S(2)}) copy-start(u32[16]{0:T(128)} %constant.29) | copy-start | bytes 196
  26.2 6.9 %copy-start.13 = (bf16[2,192]{1,0:T(2,128)(2,1)S(1)}, bf16[2,192]{1,0:T(2,128)(2,1)}, u32[]{:S(2)}) copy-start(bf16[2,192]{1,0:T(2,128)(2,1)} %param.11) | copy-start | bytes 2308
  26.2 7.2 %copy-start.14 = (bf16[2,192]{1,0:T(2,128)(2,1)S(1)}, bf16[2,192]{1,0:T(2,128)(2,1)}, u32[]{:S(2)}) copy-start(bf16[2,192]{1,0:T(2,128)(2,1)} %param.16) | copy-start | bytes 2308
  26.2 75.1 %copy-start.11 = (bf16[2,192,2,128]{3,2,1,0:T(2,128)(2,1)S(1)}, bf16[2,192,2,128]{3,2,1,0:T(2,128)(2,1)}, u32[]{:S(2)}) copy-start(bf16[2,192,2,128]{3,2,1,0:T(2,128)(2,1)} %param.13) | copy-start | bytes 589828
  26.2 75.9 %copy-start.3 = (bf16[1,64,1536]{2,1,0:T(8,128)(2,1)S(1)}, bf16[1,64,1536]{2,1,0:T(8,128)(2,1)}, u32[]{:S(2)}) copy-start(bf16[1,64,1536]{2,1,0:T(8,128)(2,1)} %param.10) | copy-start | bytes 589828
  26.2 89.1 %copy-start.12 = (bf16[2,192,2,128]{3,2,1,0:T(2,128)(2,1)S(1)}, bf16[2,192,2,128]{3,2,1,0:T(2,128)(2,1)}, u32[]{:S(2)}) copy-start(bf16[2,192,2,128]{3,2,1,0:T(2,128)(2,1)} %param.14) | copy-start | bytes 589828
  26.3 126.4 %all-to-all-start = ((bf16[8,192,1120]{2,1,0:T(8,128)(2,1)}), bf16[8,192,1120]{2,1,0:T(8,128)(2,1)}, u32[]{:S(2)}, u32[]{:S(2)}) async-start(bf16[8,192,1120]{2,1,0:T(8,128)(2,1)} %bitcast.209), calls=%async_computation | async-start | bytes 7077888 | tf_op jit(solution)/shard_map/all_to_all | solution.py:68
  31.9 126.5 %all-gather.25.cloned.1.call-start = ((), (), s32[]{:S(2)}) async-start(), calls=%async_computation.10 | async-start | bytes 1769472 | tf_op jit(solution)/shard_map/all_gather | solution.py:49
  126.5 3.7 copy-start.5
  126.5 3.7 copy-start.7
  135.1 0.7 copy-start
  152.7 45.7 %all-to-all-start.1 = ((bf16[8,192,1120]{2,1,0:T(8,128)(2,1)}), bf16[8,192,1120]{2,1,0:T(8,128)(2,1)S(1)}, u32[]{:S(2)}, u32[]{:S(2)}) async-start(bf16[8,192,1120]{2,1,0:T(8,128)(2,1)} %bitcast.208), calls=%async_computation.1 | async-start | bytes 7077888 | tf_op jit(solution)/shard_map/all_to_all | solution.py:68
  156.3 137.8 %reduce-scatter.3.cloned.1.call-start = ((), (), s32[]{:S(2)}) async-start(), calls=%async_computation.6 | async-start | bytes 3538944 | tf_op jit(solution)/shard_map/reduce_scatter | solution.py:54
  207.5 104.1 %all-gather.27.cloned.1.call-start = ((), (), s32[]{:S(2)}) async-start(), calls=%async_computation.11 | async-start | bytes 5308416 | tf_op jit(solution)/shard_map/all_gather | solution.py:72
  208.1 140.0 %all-gather.29.cloned.1.call-start = ((), (), s32[]{:S(2)}) async-start(), calls=%async_computation.12 | async-start | bytes 5308416 | tf_op jit(solution)/shard_map/all_gather | solution.py:72
  218.4 4.7 %copy-start.10 = (bf16[1,192,2,128]{3,2,1,0:T(2,128)(2,1)S(1)}, bf16[1,192,2,128]{3,2,1,0:T(2,128)(2,1)}, u32[]{:S(2)}) copy-start(bf16[1,192,2,128]{3,2,1,0:T(2,128)(2,1)} %get-tuple-element.27) | copy-start | bytes 294916
  218.4 64.2 %copy-start.9 = (bf16[1,192,2,128]{3,2,0,1:T(2,128)(2,1)S(1)}, bf16[1,192,2,128]{3,2,0,1:T(2,128)(2,1)}, u32[]{:S(2)}) copy-start(bf16[1,192,2,128]{3,2,0,1:T(2,128)(2,1)} %get-tuple-element.30) | copy-start | bytes 294916
  218.4 75.8 %copy-start.1 = (f32[1,64,1536]{2,1,0:T(8,128)S(1)}, f32[1,64,1536]{2,1,0:T(8,128)}, u32[]{:S(2)}) copy-start(f32[1,64,1536]{2,1,0:T(8,128)} %copy-done) | copy-start | bytes 1179652
  218.4 144.4 %all-to-all-start.2 = ((bf16[8,192,1120]{2,1,0:T(8,128)(2,1)}), bf16[8,192,1120]{2,1,0:T(8,128)(2,1)}, u32[]{:S(2)}, u32[]{:S(2)}) async-start(bf16[8,192,1120]{2,1,0:T(8,128)(2,1)} %bitcast.207), calls=%async_computation.3 | async-start | bytes 7077888 | tf_op jit(solution)/shard_map/all_to_all | solution.py:68
  223.1 72.6 %copy-start.6 = (f32[64,64]{1,0:T(8,128)S(1)}, f32[64,64]{1,0:T(8,128)}, u32[]{:S(2)}) copy-start(f32[64,64]{1,0:T(8,128)} %copy-done.5) | copy-start | bytes 49156
  223.1 72.6 %copy-start.8 = (f32[64,64]{1,0:T(8,128)S(1)}, f32[64,64]{1,0:T(8,128)}, u32[]{:S(2)}) copy-start(f32[64,64]{1,0:T(8,128)} %copy-done.7) | copy-start | bytes 49156
  223.1 155.9 %all-gather.31.cloned.1.call-start = ((), (), s32[]{:S(2)}) async-start(), calls=%async_computation.13 | async-start | bytes 1769472 | tf_op jit(solution)/shard_map/all_gather | solution.py:49
  351.5 0.8 copy-start.2
  362.8 49.6 %all-to-all-start.3 = ((bf16[8,192,1120]{2,1,0:T(8,128)(2,1)}), bf16[8,192,1120]{2,1,0:T(8,128)(2,1)S(1)}, u32[]{:S(2)}, u32[]{:S(2)}) async-start(bf16[8,192,1120]{2,1,0:T(8,128)(2,1)} %bitcast.206), calls=%async_computation.4 | async-start | bytes 7077888 | tf_op jit(solution)/shard_map/all_to_all | solution.py:68
  366.5 94.5 %reduce-scatter.5.cloned.1.call-start = ((), (), s32[]{:S(2)}) async-start(), calls=%async_computation.7 | async-start | bytes 3538944 | tf_op jit(solution)/shard_map/reduce_scatter | solution.py:54
Sparse Core Ops, SparseCore 0:
  9.2 57.8 all-gather.20
  68.9 46.4 all-gather.22
  136.8 21.5 all-gather.24
  207.6 61.7 reduce-scatter.2
  271.1 40.4 all-gather.26
  313.3 34.7 all-gather.28
  353.2 25.7 all-gather.30
  421.7 39.2 reduce-scatter.4

commit v2 on v0

v2 whole, which is shorter than its diff:
```python
import functools

import jax
import jax.numpy as jnp
from jax import lax
from jax.experimental import pallas as pl
from jax.experimental.pallas import tpu as pltpu
from jax.sharding import PartitionSpec as P

MESH = pl.DeviceIdType.MESH
ROPE_THETA = 500000.0
NORM_EPS = 1e-5
LAYERS = 2
SEQ = 64
DIM = 1536
HEADS = 12
KV_HEADS = 2
HEAD_DIM = 128
GROUP = HEADS // KV_HEADS
QKV = (HEADS + 2 * KV_HEADS) * HEAD_DIM
ATTN = QKV + DIM
FFN = 8960
ROWS = DIM // 8
FFN_ROWS = FFN // 8
WINDOW = 1280
HALF = ROWS // 2
DIRECT = 112
RELAY = ROWS - DIRECT
BF = jnp.bfloat16
F32 = jnp.float32
CHIPS = (2, 4, 6)
GU_ORDER = (2, 4, 6, 3, 5, 7, 1)
GU_RELAYED = (2, 4, 6, 3, 5, 7)


def aligned(value, size):
    return pl.multiple_of(value, size)


def kernel(x_ref, gain_ref, cos_ref, sin_ref, wa_ref, wg_ref, wu_ref, wd_ref, y_ref,
           gains, gain_rows, wa, wgu, wd, res, mid, q_buf, k_buf, v_buf, o_buf, u_buf, z_buf, part, r1, r2a, r2b, r3a, r3b,
           gain_s, gain_r, ad_s, ad_r, az_s, az_r, ac_s, ac_r, gd_s, gd_r, gz_s, gz_r, ag_s, ag_r, rs_s, rs_r, own_a, own_gu, own_wd):
    z = lax.axis_index("dp")
    me = lax.axis_index("fsdp")
    c = me % 2
    x = (me // 2) % 2
    y = me // 4

    def peer(k):
        cc = 1 - c if k % 2 else c
        xx = 1 - x if (k // 2) % 2 else x
        yy = 1 - y if k // 4 else y
        return 4 * yy + 2 * xx + cc

    def block(k):
        cc = 1 - c if k % 2 else c
        xx = 1 - x if (k // 2) % 2 else x
        yy = 1 - y if k // 4 else y
        return 4 * cc + 2 * yy + xx

    def window(j):
        return aligned(128 * ((35 * j) // 4 - j // 7), 128)

    def plane(k):
        return (z, peer(k))

    across = (1 - z, me)
    started = []

    def remote(src, dst, send, recv, device):
        return pltpu.make_async_remote_copy(src_ref=src, dst_ref=dst, send_sem=send, recv_sem=recv, device_id=device, device_id_type=MESH)

    def go(copy):
        copy.start()
        started.append(copy)

    barrier = pltpu.get_barrier_semaphore()
    for k in range(1, 8):
        pl.semaphore_signal(barrier, inc=1, device_id=plane(k), device_id_type=MESH)
    pl.semaphore_signal(barrier, inc=1, device_id=across, device_id_type=MESH)
    pl.semaphore_wait(barrier, 8)

    def gain_copy(k):
        return remote(gain_ref, gains.at[me], gain_s.at[k - 1], gain_r.at[k - 1], plane(k))

    def gain_arrival(k):
        dst = gains.at[peer(k)]
        return remote(dst, dst, gain_s.at[k - 1], gain_r.at[k - 1], plane(k))

    def attn_rows(l, k, half):
        return wa.at[l, pl.ds(aligned(ROWS * peer(k) + HALF * half, 32), HALF), :]

    def attn_direct(l, n):
        src = wa_ref.at[l, pl.ds(aligned(HALF * z, 32), HALF), :]
        return remote(src, attn_rows(l, 0, z), ad_s.at[l, n], ad_r.at[l, n], plane(CHIPS[n]))

    def attn_arrival(l, n):
        dst = attn_rows(l, CHIPS[n], z)
        return remote(dst, dst, ad_s.at[l, n], ad_r.at[l, n], plane(CHIPS[n]))

    def attn_across(l, n):
        rows = attn_rows(l, CHIPS[n], z)
        return remote(rows, rows, az_s.at[l, n], az_r.at[l, n], across)

    def attn_across_arrival(l, n):
        dst = attn_rows(l, CHIPS[n], 1 - z)
        return remote(dst, dst, az_s.at[l, n], az_r.at[l, n], across)

    def attn_core(l, n, half, slot):
        rows = attn_rows(l, CHIPS[n], half)
        return remote(rows, rows, ac_s.at[l, slot], ac_r.at[l, slot], plane(1))

    def attn_core_arrival(l, n, half, slot):
        dst = attn_rows(l, CHIPS[n] + 1, half)
        return remote(dst, dst, ac_s.at[l, slot], ac_r.at[l, slot], plane(1))

    def shard_rows(l, k):
        return wa.at[l, pl.ds(aligned(ROWS * peer(k), 64), ROWS), :]

    def attn_shard(l):
        return remote(wa_ref.at[l], shard_rows(l, 0), ac_s.at[l, 6], ac_r.at[l, 6], plane(1))

    def attn_shard_arrival(l):
        dst = shard_rows(l, 1)
        return remote(dst, dst, ac_s.at[l, 6], ac_r.at[l, 6], plane(1))

    def attn_own(l):
        return pltpu.make_async_copy(wa_ref.at[l], shard_rows(l, 0), own_a.at[l])

    def send_attn(l):
        for n in range(3):
            go(attn_direct(l, n))
        go(attn_shard(l))
        attn_own(l).start()

    def relay_attn(l, n):
        attn_arrival(l, n).wait_recv()
        go(attn_across(l, n))
        go(attn_core(l, n, z, n))

    def relay_attn_across(l, n):
        attn_across_arrival(l, n).wait_recv()
        go(attn_core(l, n, 1 - z, 3 + n))

    def await_attn(l):
        attn_own(l).wait()
        attn_shard_arrival(l).wait_recv()
        for n in range(3):
            attn_core_arrival(l, n, z, n).wait_recv()
        for n in range(3):
            attn_core_arrival(l, n, 1 - z, 3 + n).wait_recv()

    halves = (wg_ref, wu_ref)

    def gu_rows(l, g, k, start, count):
        return wgu.at[l, g, pl.ds(aligned(ROWS * peer(k) + start, 16), count), :]

    def gu_direct(l, g, k):
        start, count = (0, ROWS) if k == 1 else (aligned(RELAY * z, 16), DIRECT)
        src = halves[g].at[l, pl.ds(start, count), pl.ds(window(peer(k)), WINDOW)]
        return remote(src, gu_rows(l, g, 0, start, count), gd_s.at[l, g, k - 1], gd_r.at[l, g, k - 1], plane(k))

    def gu_arrival(l, g, k):
        start, count = (0, ROWS) if k == 1 else (RELAY * z, DIRECT)
        dst = gu_rows(l, g, k, start, count)
        return remote(dst, dst, gd_s.at[l, g, k - 1], gd_r.at[l, g, k - 1], plane(k))

    def gu_across(l, g, k):
        rows = gu_rows(l, g, k, DIRECT * z, RELAY)
        return remote(rows, rows, gz_s.at[l, g, k - 2], gz_r.at[l, g, k - 2], across)

    def gu_across_arrival(l, g, k):
        dst = gu_rows(l, g, k, DIRECT * (1 - z), RELAY)
        return remote(dst, dst, gz_s.at[l, g, k - 2], gz_r.at[l, g, k - 2], across)

    def gu_own(l, g):
        return pltpu.make_async_copy(halves[g].at[l, :, pl.ds(window(me), WINDOW)], gu_rows(l, g, 0, 0, ROWS), own_gu.at[l, g])

    def send_gu(l):
        for k in GU_ORDER:
            for g in range(2):
                go(gu_direct(l, g, k))
        for g in range(2):
            gu_own(l, g).start()

    def relay_gu(l, k):
        for g in range(2):
            gu_arrival(l, g, k).wait_recv()
            go(gu_across(l, g, k))

    def await_gu(l):
        for g in range(2):
            gu_arrival(l, g, 1).wait_recv()
            gu_own(l, g).wait()
        for k in GU_RELAYED:
            for g in range(2):
                gu_across_arrival(l, g, k).wait_recv()

    skip = FFN_ROWS * me - window(me)

    def wd_copy(l):
        return pltpu.make_async_copy(wd_ref.at[l], wd.at[pl.ds(aligned(skip, 32), FFN_ROWS), :], own_wd)

    def normed(ref, row):
        wide = ref[...].astype(F32)
        inv_rms = lax.rsqrt(jnp.mean(wide * wide, axis=-1, keepdims=True) + NORM_EPS)
        return (wide * inv_rms * gain_rows[row : row + 1, :]).astype(BF)

    def project(l):
        u = normed(res, l)
        cos, sin = cos_ref[...], sin_ref[...]

        def rotate(v):
            return (v * cos + pltpu.roll(v, HEAD_DIM // 2, 1) * sin).astype(BF)

        def two_heads(n):
            return jnp.dot(u, wa[l, :, pl.ds(aligned(256 * n, 256), 256)], preferred_element_type=F32)

        def q_heads(n, carry):
            pair = two_heads(n)
            for t in range(2):
                q_buf[pl.ds(aligned((2 * n + t) * SEQ, SEQ), SEQ), :] = rotate(pair[:, 128 * t : 128 * (t + 1)])
            return carry

        lax.fori_loop(0, HEADS // 2, q_heads, 0)
        keys, values = two_heads(HEADS // 2), two_heads(HEADS // 2 + 1)
        for t in range(2):
            k_buf[t] = rotate(keys[:, 128 * t : 128 * (t + 1)])
            v_buf[t] = values[:, 128 * t : 128 * (t + 1)].astype(BF)

    def attend(l):
        row = lax.broadcasted_iota(jnp.int32, (GROUP * SEQ, SEQ), 0) % SEQ
        col = lax.broadcasted_iota(jnp.int32, (GROUP * SEQ, SEQ), 1)
        for g in range(KV_HEADS):
            q = q_buf[g * GROUP * SEQ : (g + 1) * GROUP * SEQ, :]
            scores = lax.dot_general(q, k_buf[g], (((1,), (1,)), ((), ())), preferred_element_type=F32) * HEAD_DIM ** -0.5
            scores = jnp.where(row >= col, scores, -jnp.inf)
            e = jnp.exp(scores - jnp.max(scores, axis=-1, keepdims=True))
            probs = (e / jnp.sum(e, axis=-1, keepdims=True)).astype(BF)
            o = jnp.dot(probs, v_buf[g], preferred_element_type=F32).astype(BF)
            for j in range(GROUP):
                h = g * GROUP + j
                o_buf[:, h * HEAD_DIM : (h + 1) * HEAD_DIM] = o[j * SEQ : (j + 1) * SEQ]

        def out_cols(n, carry):
            cols = pl.ds(aligned(256 * n, 256), 256)
            add = jnp.dot(o_buf[...], wa[l, :, pl.ds(aligned(QKV + 256 * n, 256), 256)], preferred_element_type=F32)
            mid[:, cols] = (res[:, cols].astype(F32) + add).astype(BF)
            return carry

        lax.fori_loop(0, DIM // 256, out_cols, 0)

    def seq_rows(l, k):
        return u_buf.at[l, pl.ds(aligned(SEQ * block(k), SEQ), SEQ), :]

    def ag_copy(l, k):
        return remote(seq_rows(l, 0), seq_rows(l, 0), ag_s.at[l, k - 1], ag_r.at[l, k - 1], plane(k))

    def ag_relay(l, k):
        return remote(seq_rows(l, k), seq_rows(l, k), ag_s.at[l, k], ag_r.at[l, k], plane(1))

    def ag_arrival(l, k):
        dst = seq_rows(l, k)
        return remote(dst, dst, ag_s.at[l, k - 1], ag_r.at[l, k - 1], plane(k))

    def gate_up(l, b):
        rows = pl.ds(aligned(256 * b, 256), 256)

        def cols(n, carry):
            at = pl.ds(aligned(256 * n, 256), 256)
            u = u_buf[l, rows, :]
            gate = jnp.dot(u, wgu[l, 0, :, at], preferred_element_type=F32).astype(BF).astype(F32)
            up = jnp.dot(u, wgu[l, 1, :, at], preferred_element_type=F32).astype(BF).astype(F32)
            gated = (jax.nn.silu(gate) * up).astype(BF)
            place = 256 * n + lax.broadcasted_iota(jnp.int32, (256, 256), 1)
            mine = (place >= skip) & (place < skip + FFN_ROWS)
            z_buf[rows, at] = jnp.where(mine, gated, jnp.zeros_like(gated))
            return carry

        lax.fori_loop(0, WINDOW // 256, cols, 0)

    def down(b):
        rows = pl.ds(aligned(256 * b, 256), 256)

        def cols(n, carry):
            at = pl.ds(aligned(256 * n, 256), 256)
            part[b, :, at] = jnp.dot(z_buf[rows, :], wd[:, at], preferred_element_type=F32)
            return carry

        lax.fori_loop(0, DIM // 256, cols, 0)

    A, B = slice(0, DIM // 2), slice(DIM // 2, DIM)

    def chip_rows(yy, xx):
        return pl.ds(aligned(SEQ * (2 * yy + xx), SEQ), SEQ)

    def rs_core(l):
        return remote(part.at[1 - c], r1.at[l], rs_s.at[l, 0], rs_r.at[l, 0], plane(1))

    def rs_a(l, yy):
        return remote(part.at[c, chip_rows(yy, 1 - x), A], r2a.at[l, yy], rs_s.at[l, 1 + yy], rs_r.at[l, 1 + yy], plane(2))

    def rs_b(l, xx):
        return remote(part.at[c, chip_rows(1 - y, xx), B], r2b.at[l, xx], rs_s.at[l, 3 + xx], rs_r.at[l, 3 + xx], plane(4))

    def rs_a_last(l):
        return remote(part.at[c, chip_rows(1 - y, x), A], r3a.at[l], rs_s.at[l, 5], rs_r.at[l, 5], plane(4))

    def rs_b_last(l):
        return remote(part.at[c, chip_rows(y, 1 - x), B], r3b.at[l], rs_s.at[l, 6], rs_r.at[l, 6], plane(2))

    for k in range(1, 8):
        go(gain_copy(k))
    send_attn(0)
    send_gu(0)
    gains[me] = gain_ref[...]
    res[...] = x_ref[...]

    def clear(n, carry):
        wd[pl.ds(aligned(128 * n, 128), 128), :] = jnp.zeros((128, DIM), BF)
        return carry

    lax.fori_loop(0, WINDOW // 128, clear, 0)
    for k in range(1, 8):
        gain_arrival(k).wait_recv()
    for p in range(4):
        gain_rows[:, 384 * p : 384 * (p + 1)] = gains[2 * p] + gains[2 * p + 1]
    for n in range(3):
        relay_attn(0, n)

    for l in range(LAYERS):
        wd_copy(l).start()
        for n in range(3):
            relay_attn_across(l, n)
        await_attn(l)
        for k in GU_RELAYED[:1]:
            relay_gu(l, k)
        project(l)
        for k in GU_RELAYED[1:2]:
            relay_gu(l, k)
        attend(l)
        u_buf[l, pl.ds(aligned(SEQ * block(0), SEQ), SEQ), :] = normed(mid, 2 + l)
        for k in (2, 4, 6, 1):
            go(ag_copy(l, k))
        if l + 1 < LAYERS:
            send_attn(l + 1)
        for k in GU_RELAYED[2:]:
            relay_gu(l, k)
        for k in CHIPS:
            ag_arrival(l, k).wait_recv()
            go(ag_relay(l, k))
        await_gu(l)
        gate_up(l, c)
        for k in (1, 3, 5, 7):
            ag_arrival(l, k).wait_recv()
        gate_up(l, 1 - c)
        wd_copy(l).wait()
        down(1 - c)
        to_core = rs_core(l)
        to_core.start()
        down(c)
        to_core.wait_recv()
        part[c] = part[c] + r1[l]
        sends = [to_core]
        for t in range(2):
            for copy in (rs_a(l, t), rs_b(l, t)):
                copy.start()
                sends.append(copy)
        if l + 1 < LAYERS:
            for n in range(3):
                relay_attn(l + 1, n)
        for t in range(2):
            rs_a(l, t).wait_recv()
            rs_b(l, t).wait_recv()
            part[c, chip_rows(t, x), A] = part[c, chip_rows(t, x), A] + r2a[l, t]
            part[c, chip_rows(y, t), B] = part[c, chip_rows(y, t), B] + r2b[l, t]
        for copy in (rs_a_last(l), rs_b_last(l)):
            copy.start()
            sends.append(copy)
        if l + 1 < LAYERS:
            send_gu(l + 1)
        rs_a_last(l).wait_recv()
        rs_b_last(l).wait_recv()
        out = y_ref if l + 1 == LAYERS else res
        out[:, A] = (mid[:, A].astype(F32) + (part[c, chip_rows(y, x), A] + r3a[l])).astype(BF)
        out[:, B] = (mid[:, B].astype(F32) + (part[c, chip_rows(y, x), B] + r3b[l])).astype(BF)
        for copy in sends:
            copy.wait_send()
    for copy in started:
        copy.wait_send()


def solution(mesh):
    vmem = pl.BlockSpec(memory_space=pltpu.VMEM)
    hbm = pl.BlockSpec(memory_space=pl.ANY)
    dma = pltpu.SemaphoreType.DMA

    def local_forward(hidden, attn_norm, w_q, w_k, w_v, w_o, mlp_norm, w_gate, w_up, w_down):
        me = lax.axis_index("fsdp")
        gain = jnp.concatenate([attn_norm, mlp_norm, jnp.zeros((4, ROWS), BF)], axis=0).astype(F32)
        gain = jnp.where(me % 2 == 0, jnp.pad(gain, ((0, 0), (0, ROWS))), jnp.pad(gain, ((0, 0), (ROWS, 0))))
        inv_freq = jnp.power(ROPE_THETA, -(jnp.arange(HEAD_DIM // 2, dtype=F32) * 2.0 / HEAD_DIM))
        angles = jnp.arange(SEQ, dtype=F32)[:, None] * inv_freq[None, :]
        cos = jnp.concatenate([jnp.cos(angles), jnp.cos(angles)], axis=1)
        sin = jnp.concatenate([-jnp.sin(angles), jnp.sin(angles)], axis=1)
        flat = [w.reshape(LAYERS, ROWS, -1) for w in (w_q, w_k, w_v, w_o)]
        attn = jnp.concatenate(flat, axis=2)
        y = pl.pallas_call(
            kernel,
            out_shape=jax.ShapeDtypeStruct((SEQ, DIM), BF),
            in_specs=[vmem] * 4 + [hbm] * 4,
            out_specs=vmem,
            scratch_shapes=[
                pltpu.VMEM((8, 8, 2 * ROWS), F32),
                pltpu.VMEM((8, DIM), F32),
                pltpu.VMEM((LAYERS, DIM, ATTN), BF),
                pltpu.VMEM((LAYERS, 2, DIM, WINDOW), BF),
                pltpu.VMEM((WINDOW, DIM), BF),
                pltpu.VMEM((SEQ, DIM), BF),
                pltpu.VMEM((SEQ, DIM), BF),
                pltpu.VMEM((HEADS * SEQ, HEAD_DIM), BF),
                pltpu.VMEM((KV_HEADS, SEQ, HEAD_DIM), BF),
                pltpu.VMEM((KV_HEADS, SEQ, HEAD_DIM), BF),
                pltpu.VMEM((SEQ, DIM), BF),
                pltpu.VMEM((LAYERS, 8 * SEQ, DIM), BF),
                pltpu.VMEM((8 * SEQ, WINDOW), BF),
                pltpu.VMEM((2, 4 * SEQ, DIM), F32),
                pltpu.VMEM((LAYERS, 4 * SEQ, DIM), F32),
                pltpu.VMEM((LAYERS, 2, SEQ, DIM // 2), F32),
                pltpu.VMEM((LAYERS, 2, SEQ, DIM // 2), F32),
                pltpu.VMEM((LAYERS, SEQ, DIM // 2), F32),
                pltpu.VMEM((LAYERS, SEQ, DIM // 2), F32),
                dma((7,)), dma((7,)),
                dma((LAYERS, 3)), dma((LAYERS, 3)),
                dma((LAYERS, 3)), dma((LAYERS, 3)),
                dma((LAYERS, 7)), dma((LAYERS, 7)),
                dma((LAYERS, 2, 7)), dma((LAYERS, 2, 7)),
                dma((LAYERS, 2, 6)), dma((LAYERS, 2, 6)),
                dma((LAYERS, 7)), dma((LAYERS, 7)),
                dma((LAYERS, 7)), dma((LAYERS, 7)),
                dma((LAYERS,)), dma((LAYERS, 2)), dma(()),
            ],
            compiler_params=pltpu.CompilerParams(collective_id=0, has_side_effects=True, vmem_limit_bytes=67043328),
        )(hidden.reshape(SEQ, DIM), gain, cos, sin, attn, w_gate, w_up, w_down)
        return y.reshape(1, SEQ, DIM)

    batch_spec = P(("dp", "fsdp"), None, None)
    gain_spec = P(None, "fsdp")
    proj_spec = P(None, "fsdp", None, None)
    mat_spec = P(None, "fsdp", None)
    return jax.shard_map(local_forward, mesh=mesh, in_specs=(batch_spec, gain_spec, proj_spec, proj_spec, proj_spec, mat_spec, gain_spec, mat_spec, mat_spec, mat_spec), out_specs=batch_spec, check_vma=False)
```

time: 991 us -> 273 us (0.28)
  waiting for transfers between devices: 793 us -> 0 us
  Pallas kernels: 0 us -> 264 us
  matrix products: 81.2 us -> 0 us
  blocking collectives: 75.2 us -> 0 us
  local copies, waits for them, and re-layouts: 25 us -> 5.21 us
  between operations: 14.6 us -> 0.03 us
    all_gather x10 -> x0, waiting for transfers between devices: 790 us -> none  [local_forward(): lax.all_gather(shard[layer], 'fsdp', axis=0, tiled=True)]
    pallas_call x0 -> x1, Pallas kernels: none -> 264 us  [local_forward(): pl.pallas_call(kernel, out_shape=jax.ShapeDtypeStruct((SEQ, DIM), BF), in...]
    dot_general x14 -> x0, matrix products: 81.2 us -> none  [the longest x2 41.5 us: decoder_layer(): jnp.einsum('bsf,fd->bsd', gated, w_down, preferred_element_type=jnp.float32)]
    all_gather x4 -> x0, blocking collectives: 49 us -> none  [local_forward(): lax.all_gather(shard[layer], 'fsdp', axis=0, tiled=True)]
    unnamed x1 -> x0, blocking collectives: 26.1 us -> none
    slice x8 -> x0, local copies, waits for them, and re-layouts: 22.5 us -> none  [local_forward(): shard[layer]]
  transfers between devices with their start and end apart: 10 -> 0, of which waited for: 8 -> 0; matrix products, arithmetic and copies ran while one was open for 8% -> 0% of each run, Pallas kernels for 0% -> 0%
where the time goes in v2:
time: 273 us
  Pallas kernels  264 us (97%)
  local copies, waits for them, and re-layouts  5.21 us (2%)
  other arithmetic  4.06 us (1%)
    pallas_call x1, Pallas kernels, local_forward(): pl.pallas_call(kernel, out_shape=jax.ShapeDtypeStruct((SEQ, DIM), BF), in...  264 us

profile of v2, /device:TPU:0, one launch (start us, length us, event | category | flops | bytes accessed | tf_op | source)
XLA Modules:
  0.0 273.1 jit_solution(16400796903465624937)
XLA Ops:
  0.0 0.0 copy-start
  0.0 0.1 pad.20.clone
  0.1 0.8 maximum_convert_fusion
  0.9 0.7 pad_select_fusion.gain_ref
  1.6 0.1 fusion.2
  1.8 0.7 pad_maximum_fusion.1
  2.5 1.1 reshape.23
  3.5 1.1 reshape.24
  4.6 1.4 copy_bitcast_fusion
  6.0 0.0 copy-done
  6.0 1.7 pad_maximum_fusion.wa_ref
  7.7 263.8 %shard_map.100 = bf16[64,1536]{1,0:T(8,128)(2,1)} custom-call(bf16[64,1536]{1,0:T(8,128)(2,1)} %bitcast.8, f32[8,384]{1,0:T(8,128)} %pad_select_fusion.gain_ref, f32[64,128]{1,0:T(8,128)} %get-tuple-element.8.cos_ref, f32[64,128]{1,0:T(8,128)} %get-tuple-element.9.sin_ref, bf16[2,192,3584]{2,1,0:T(8,128)(2,1)} %pad_maximum_fusion.wa_ref, ...), custom_call_target="tpu_custom_call" | custom-call | tf_op jit(solution)/shard_map/pallas_call | solution.py:408
  271.5 1.6 copy.16
  (2 shorter events, 0.0 us)
Async XLA Ops:
  0.0 6.0 %copy-start = (bf16[2,192,1536]{2,1,0:T(8,128)(2,1)S(1)}, bf16[2,192,1536]{2,1,0:T(8,128)(2,1)}, u32[]{:S(2)}) copy-start(bf16[2,192,1536]{2,1,0:T(8,128)(2,1)} %param.15) | copy-start | bytes 3538948

commit v3 on v2

v3 whole, which is shorter than its diff:
```python
import functools

import jax
import jax.numpy as jnp
import numpy as np
from jax import lax
from jax.experimental import pallas as pl
from jax.experimental.pallas import tpu as pltpu
from jax.sharding import PartitionSpec as P

MESH = pl.DeviceIdType.MESH
ROPE_THETA = 500000.0
NORM_EPS = 1e-5
LAYERS = 2
SEQ = 64
DIM = 1536
HEADS = 12
KV_HEADS = 2
HEAD_DIM = 128
GROUP = HEADS // KV_HEADS
GROUP_COLS = (GROUP + 2) * HEAD_DIM
OUT_COLS = DIM // 2
FFN = 8960
ROWS = DIM // 8
FFN_ROWS = FFN // 8
WINDOW = 1152
MAIN = 1088
EDGE = 32
HALF = ROWS // 2
DIRECT = 112
RELAY = ROWS - DIRECT
BF = jnp.bfloat16
F32 = jnp.float32
CHIPS = (2, 4, 6)
PARTS = ((0, 768), (768, 384))
GU_RELAYED = (2, 4, 6, 3, 5, 7)
RELAYS = (((2, 0), (4, 0)), ((2, 1), (4, 1)), ((6, 0), (6, 1), (3, 0), (5, 0)), ((3, 1), (5, 1), (7, 0), (7, 1)))
GU_EARLY = ((2, 0), (4, 0))
GU_LATE = ((2, 1), (4, 1), (6, 0), (6, 1), (3, 0), (5, 0), (3, 1), (5, 1), (7, 0), (7, 1), (1, 0), (1, 1))


def aligned(value, size):
    return pl.multiple_of(value, size)


def kernel(x_ref, an_ref, mn_ref, cos_ref, sin_ref, wqkv_ref, wo_ref, wg_ref, wu_ref, wd_ref, y_ref,
           gain_mine, gains, gain_rows, wq, wo, wgu, wd, edge, res, mid, n_buf, q_buf, k_buf, v_buf, o_buf, add_mine, add_got, u_buf, z_buf, part,
           r1, r2a, r2b, r3a, r3b,
           gain_s, gain_r, ad_s, ad_r, ax_s, ax_r, ac_s, ac_r, zx_s, zx_r, gd_s, gd_r, gz_s, gz_r, ed_s, ed_r, ag_s, ag_r, rs_s, rs_r,
           own_a, own_gu, own_wd):
    z = lax.axis_index("dp")
    me = lax.axis_index("fsdp")
    c = me % 2
    x = (me // 2) % 2
    y = me // 4

    def peer(k):
        cc = 1 - c if k % 2 else c
        xx = 1 - x if (k // 2) % 2 else x
        yy = 1 - y if k // 4 else y
        return 4 * yy + 2 * xx + cc

    def block(k):
        cc = 1 - c if k % 2 else c
        xx = 1 - x if (k // 2) % 2 else x
        yy = 1 - y if k // 4 else y
        return 4 * cc + 2 * yy + xx

    def window(j):
        return aligned(128 * (35 * (j // 4) + 9 * (j % 4) - (j % 4) // 2), 128)

    def plane(k):
        return (z, peer(k))

    across = (1 - z, me)
    started = []

    def remote(src, dst, send, recv, device):
        return pltpu.make_async_remote_copy(src_ref=src, dst_ref=dst, send_sem=send, recv_sem=recv, device_id=device, device_id_type=MESH)

    def go(copy):
        copy.start()
        started.append(copy)

    barrier = pltpu.get_barrier_semaphore()
    for k in range(1, 8):
        pl.semaphore_signal(barrier, inc=1, device_id=plane(k), device_id_type=MESH)
    pl.semaphore_signal(barrier, inc=1, device_id=across, device_id_type=MESH)
    pl.semaphore_wait(barrier, 8)

    def gain_copy(k):
        return remote(gain_mine, gains.at[me], gain_s.at[k - 1], gain_r.at[k - 1], plane(k))

    def gain_arrival(k):
        dst = gains.at[peer(k)]
        return remote(dst, dst, gain_s.at[k - 1], gain_r.at[k - 1], plane(k))

    attn_src = (wqkv_ref, wo_ref)
    attn_dst = (wq, wo)
    attn_cols = (GROUP_COLS, OUT_COLS)

    def attn_rows(l, m, k, start=0, count=ROWS):
        return attn_dst[m].at[l, pl.ds(aligned(ROWS * peer(k) + start, 32), count), :]

    def attn_shard(l, m):
        return attn_src[m].at[l, :, pl.ds(aligned(attn_cols[m] * z, 128), attn_cols[m])]

    def attn_own(l, m):
        return pltpu.make_async_copy(attn_shard(l, m), attn_rows(l, m, 0), own_a.at[l, m])

    def attn_direct(l, m, n):
        return remote(attn_shard(l, m), attn_rows(l, m, 0), ad_s.at[l, m, n], ad_r.at[l, m, n], plane(2 + 2 * n))

    def attn_arrival(l, m, n):
        dst = attn_rows(l, m, 2 + 2 * n)
        return remote(dst, dst, ad_s.at[l, m, n], ad_r.at[l, m, n], plane(2 + 2 * n))

    def attn_turn(l, m, n):
        rows = attn_rows(l, m, 2 + 2 * n, HALF * n, HALF)
        return remote(rows, rows, ax_s.at[l, m, n], ax_r.at[l, m, n], plane(4 - 2 * n))

    def attn_turn_arrival(l, m, n):
        dst = attn_rows(l, m, 6, HALF * n, HALF)
        return remote(dst, dst, ax_s.at[l, m, n], ax_r.at[l, m, n], plane(4 - 2 * n))

    def attn_core(l, m, slot, k, *part_rows):
        rows = attn_rows(l, m, k, *part_rows)
        return remote(rows, rows, ac_s.at[l, m, slot], ac_r.at[l, m, slot], plane(1))

    def attn_core_own(l, m):
        return remote(attn_shard(l, m), attn_rows(l, m, 0), ac_s.at[l, m, 0], ac_r.at[l, m, 0], plane(1))

    def send_attn(l):
        for m in range(2):
            for n in range(2):
                go(attn_direct(l, m, n))
        for m in range(2):
            go(attn_core_own(l, m))
            attn_own(l, m).start()

    def relay_attn(l):
        for m in range(2):
            for n in range(2):
                attn_arrival(l, m, n).wait_recv()
                go(attn_turn(l, m, n))
                go(attn_core(l, m, 1 + n, 2 + 2 * n))

    def relay_attn_across(l):
        for m in range(2):
            for n in range(2):
                attn_turn_arrival(l, m, n).wait_recv()
                go(attn_core(l, m, 3 + n, 6, HALF * n, HALF))

    def await_attn(l, m):
        attn_own(l, m).wait()
        attn_core(l, m, 0, 1).wait_recv()
        for n in range(2):
            attn_core(l, m, 1 + n, 3 + 2 * n).wait_recv()
            attn_core(l, m, 3 + n, 7, HALF * n, HALF).wait_recv()

    halves = (wg_ref, wu_ref)

    def gu_rows(l, p, g, k, start, count):
        return wgu.at[l, g, pl.ds(aligned(ROWS * peer(k) + start, 16), count), pl.ds(*PARTS[p])]

    def gu_direct(l, p, g, k):
        start, count = (0, ROWS) if k == 1 else (aligned(RELAY * z, 16), DIRECT)
        src = halves[g].at[l, pl.ds(start, count), pl.ds(aligned(window(peer(k)) + PARTS[p][0], 128), PARTS[p][1])]
        return remote(src, gu_rows(l, p, g, 0, start, count), gd_s.at[l, p, g, k - 1], gd_r.at[l, p, g, k - 1], plane(k))

    def gu_arrival(l, p, g, k):
        start, count = (0, ROWS) if k == 1 else (RELAY * z, DIRECT)
        dst = gu_rows(l, p, g, k, start, count)
        return remote(dst, dst, gd_s.at[l, p, g, k - 1], gd_r.at[l, p, g, k - 1], plane(k))

    def gu_across(l, p, g, k):
        rows = gu_rows(l, p, g, k, DIRECT * z, RELAY)
        return remote(rows, rows, gz_s.at[l, p, g, k - 2], gz_r.at[l, p, g, k - 2], across)

    def gu_across_arrival(l, p, g, k):
        dst = gu_rows(l, p, g, k, DIRECT * (1 - z), RELAY)
        return remote(dst, dst, gz_s.at[l, p, g, k - 2], gz_r.at[l, p, g, k - 2], across)

    def gu_own(l, g):
        dst = wgu.at[l, g, pl.ds(aligned(ROWS * me, 64), ROWS), :]
        return pltpu.make_async_copy(halves[g].at[l, :, pl.ds(window(me), WINDOW)], dst, own_gu.at[l, g])

    def send_gu(l, p, blocks):
        for k, g in blocks:
            go(gu_direct(l, p, g, k))

    def relay_gu(l, p, blocks):
        for k, g in blocks:
            gu_arrival(l, p, g, k).wait_recv()
            go(gu_across(l, p, g, k))

    def await_gu(l, p):
        for g in range(2):
            gu_arrival(l, p, g, 1).wait_recv()
            if p == 0:
                gu_own(l, g).wait()
        for k in GU_RELAYED:
            for g in range(2):
                gu_across_arrival(l, p, g, k).wait_recv()

    def start_own(l):
        for g in range(2):
            gu_own(l, g).start()
        wd_copy(l).start()
        edge_own(l).start()
        go(edge_core(l))

    def wd_copy(l):
        return pltpu.make_async_copy(wd_ref.at[l, pl.ds(aligned(EDGE * c, EDGE), MAIN), :], wd.at[l, pl.ds(aligned(2 * EDGE * x, EDGE), MAIN), :], own_wd.at[l, 0])

    def edge_own(l):
        return pltpu.make_async_copy(wd_ref.at[l, pl.ds(aligned(MAIN * (1 - x), EDGE), EDGE), :], edge.at[l, 0], own_wd.at[l, 1])

    def edge_core(l):
        return remote(wd_ref.at[l, pl.ds(aligned(MAIN * x, EDGE), EDGE), :], edge.at[l, 1], ed_s.at[l], ed_r.at[l], plane(1))

    takes = c == x

    def finish_wd(l):
        wd_copy(l).wait()
        edge_own(l).wait()
        edge_core(l).wait_recv()
        own, got = edge[l, 0], edge[l, 1]
        none = jnp.zeros_like(own)
        place = MAIN * (1 - x)
        wd[l, pl.ds(aligned(place, EDGE), EDGE), :] = jnp.where(takes, jnp.where(x == 0, own, got), none)
        wd[l, pl.ds(aligned(place + EDGE, EDGE), EDGE), :] = jnp.where(takes, jnp.where(x == 0, got, own), none)

    first = jnp.where(takes, 0, 2 * EDGE * x)
    last = jnp.where(takes, WINDOW, 2 * EDGE * x + MAIN)

    def normed(ref, row):
        wide = ref[...].astype(F32)
        inv_rms = lax.rsqrt(jnp.mean(wide * wide, axis=-1, keepdims=True) + NORM_EPS)
        return (wide * inv_rms * gain_rows[row : row + 1, :]).astype(BF)

    mine, other = pl.ds(aligned(SEQ * z, SEQ), SEQ), pl.ds(aligned(SEQ * (1 - z), SEQ), SEQ)
    left, right = pl.ds(aligned(OUT_COLS * z, 128), OUT_COLS), pl.ds(aligned(OUT_COLS * (1 - z), 128), OUT_COLS)

    def swap_in(l):
        rows = n_buf.at[l, mine, :]
        return remote(rows, rows, zx_s.at[l, 0], zx_r.at[l, 0], across)

    def swap_in_arrival(l):
        rows = n_buf.at[l, other, :]
        return remote(rows, rows, zx_s.at[l, 0], zx_r.at[l, 0], across)

    def swap_heads(l):
        cols = o_buf.at[l, :, left]
        return remote(cols, cols, zx_s.at[l, 1], zx_r.at[l, 1], across)

    def swap_heads_arrival(l):
        cols = o_buf.at[l, :, right]
        return remote(cols, cols, zx_s.at[l, 1], zx_r.at[l, 1], across)

    def swap_out(l):
        return remote(add_mine.at[l, other, :], add_got.at[l], zx_s.at[l, 2], zx_r.at[l, 2], across)

    def start_layer(l):
        n_buf[l, mine, :] = normed(res, l)
        go(swap_in(l))

    def project(l):
        cos, sin = cos_ref[...], sin_ref[...]

        def rotate(v):
            return (v * cos + pltpu.roll(v, HEAD_DIM // 2, 1) * sin).astype(BF)

        def two_heads(n):
            return jnp.dot(n_buf[l], wq[l, :, pl.ds(aligned(256 * n, 256), 256)], preferred_element_type=F32)

        def q_heads(n, carry):
            pair = two_heads(n)
            for t in range(2):
                turned = rotate(pair[:, 128 * t : 128 * (t + 1)])
                for seq in range(2):
                    q_buf[seq, pl.ds(aligned((2 * n + t) * SEQ, SEQ), SEQ), :] = turned[SEQ * seq : SEQ * (seq + 1)]
            return carry

        lax.fori_loop(0, GROUP // 2, q_heads, 0)
        pair = two_heads(GROUP // 2)
        k_buf[...] = rotate(pair[:, :128])
        v_buf[...] = pair[:, 128:].astype(BF)

    def attend(l):
        row = lax.broadcasted_iota(jnp.int32, (GROUP * SEQ, SEQ), 0) % SEQ
        col = lax.broadcasted_iota(jnp.int32, (GROUP * SEQ, SEQ), 1)
        for seq in range(2):
            rows = slice(SEQ * seq, SEQ * (seq + 1))
            scores = lax.dot_general(q_buf[seq], k_buf[rows, :], (((1,), (1,)), ((), ())), preferred_element_type=F32) * HEAD_DIM ** -0.5
            scores = jnp.where(row >= col, scores, -jnp.inf)
            e = jnp.exp(scores - jnp.max(scores, axis=-1, keepdims=True))
            probs = (e / jnp.sum(e, axis=-1, keepdims=True)).astype(BF)
            o = jnp.dot(probs, v_buf[rows, :], preferred_element_type=F32).astype(BF)
            for j in range(GROUP):
                o_buf[l, rows, pl.ds(aligned(OUT_COLS * z + HEAD_DIM * j, 128), HEAD_DIM)] = o[j * SEQ : (j + 1) * SEQ]

    def project_out(l):
        def out_cols(n, carry):
            cols = pl.ds(aligned(256 * n, 256), 256)
            add_mine[l, :, cols] = jnp.dot(o_buf[l], wo[l, :, cols], preferred_element_type=F32)
            return carry

        lax.fori_loop(0, OUT_COLS // 256, out_cols, 0)

    def finish_attn(l):
        mid[:, left] = (res[:, left].astype(F32) + add_mine[l, mine, :]).astype(BF)
        mid[:, right] = (res[:, right].astype(F32) + add_got[l]).astype(BF)

    def seq_rows(l, k):
        return u_buf.at[l, pl.ds(aligned(SEQ * block(k), SEQ), SEQ), :]

    def ag_copy(l, k):
        return remote(seq_rows(l, 0), seq_rows(l, 0), ag_s.at[l, k - 1], ag_r.at[l, k - 1], plane(k))

    def ag_relay(l, k):
        return remote(seq_rows(l, k), seq_rows(l, k), ag_s.at[l, k], ag_r.at[l, k], plane(1))

    def ag_arrival(l, k):
        dst = seq_rows(l, k)
        return remote(dst, dst, ag_s.at[l, k - 1], ag_r.at[l, k - 1], plane(k))

    def gate_up(l, p, b):
        rows = pl.ds(aligned(256 * b, 256), 256)
        begin, size = PARTS[p]

        def columns(start, width):
            at = pl.ds(aligned(start, 128), width)
            u = u_buf[l, rows, :]
            gate = jnp.dot(u, wgu[l, 0, :, at], preferred_element_type=F32).astype(BF).astype(F32)
            up = jnp.dot(u, wgu[l, 1, :, at], preferred_element_type=F32).astype(BF).astype(F32)
            gated = (jax.nn.silu(gate) * up).astype(BF)
            place = start + lax.broadcasted_iota(jnp.int32, (256, width), 1)
            valid = (place >= first) & (place < last)
            z_buf[rows, at] = jnp.where(valid, gated, jnp.zeros_like(gated))

        def cols(n, carry):
            columns(begin + 256 * n, 256)
            return carry

        lax.fori_loop(0, size // 256, cols, 0)
        if size % 256:
            columns(begin + size - 128, 128)

    def down(l, b, half):
        rows = pl.ds(aligned(256 * b, 256), 256)

        def cols(n, carry):
            at = pl.ds(aligned(256 * n, 256), 256)
            part[b, :, at] = jnp.dot(z_buf[rows, :], wd[l, :, at], preferred_element_type=F32)
            return carry

        lax.fori_loop(3 * half, 3 * half + 3, cols, 0)

    A, B = slice(0, DIM // 2), slice(DIM // 2, DIM)

    def chip_rows(yy, xx):
        return pl.ds(aligned(SEQ * (2 * yy + xx), SEQ), SEQ)

    def rs_core(l, half):
        cols = (A, B)[half]
        sem = 7 if half else 0
        return remote(part.at[1 - c, :, cols], r1.at[l, :, cols], rs_s.at[l, sem], rs_r.at[l, sem], plane(1))

    def rs_a(l, yy):
        return remote(part.at[c, chip_rows(yy, 1 - x), A], r2a.at[l, yy], rs_s.at[l, 1 + yy], rs_r.at[l, 1 + yy], plane(2))

    def rs_b(l, xx):
        return remote(part.at[c, chip_rows(1 - y, xx), B], r2b.at[l, xx], rs_s.at[l, 3 + xx], rs_r.at[l, 3 + xx], plane(4))

    def rs_a_last(l):
        return remote(part.at[c, chip_rows(1 - y, x), A], r3a.at[l], rs_s.at[l, 5], rs_r.at[l, 5], plane(4))

    def rs_b_last(l):
        return remote(part.at[c, chip_rows(y, 1 - x), B], r3b.at[l], rs_s.at[l, 6], rs_r.at[l, 6], plane(2))

    gain_mine[...] = jnp.zeros_like(gain_mine)
    gain_mine[0:LAYERS, 0:ROWS] = an_ref[...].astype(F32)
    gain_mine[LAYERS : 2 * LAYERS, 0:ROWS] = mn_ref[...].astype(F32)
    gain_mine[...] = jnp.where(c == 1, pltpu.roll(gain_mine[...], ROWS, 1), gain_mine[...])
    for k in range(1, 8):
        go(gain_copy(k))
    send_attn(0)
    send_gu(0, 0, GU_EARLY)
    gains[me] = gain_mine[...]
    res[...] = x_ref[...]
    for k in range(1, 8):
        gain_arrival(k).wait_recv()
    for p in range(4):
        gain_rows[:, 384 * p : 384 * (p + 1)] = gains[2 * p] + gains[2 * p + 1]
    start_layer(0)
    relay_attn(0)
    send_gu(0, 0, GU_LATE)
    for l in range(LAYERS):
        start_own(l)

    sends = []
    for l in range(LAYERS):
        relay_gu(l, 0, RELAYS[0])
        relay_attn_across(l)
        await_attn(l, 0)
        swap_in_arrival(l).wait_recv()
        project(l)
        attend(l)
        go(swap_heads(l))
        relay_gu(l, 0, RELAYS[1])
        await_attn(l, 1)
        swap_heads_arrival(l).wait_recv()
        project_out(l)
        go(swap_out(l))
        relay_gu(l, 0, RELAYS[2])
        swap_out(l).wait_recv()
        finish_attn(l)
        u_buf[l, pl.ds(aligned(SEQ * block(0), SEQ), SEQ), :] = normed(mid, 2 + l)
        for k in (2, 4, 6, 1):
            go(ag_copy(l, k))
        send_gu(l, 1, GU_EARLY + GU_LATE)
        if l + 1 < LAYERS:
            send_attn(l + 1)
        relay_gu(l, 0, RELAYS[3])
        for k in CHIPS:
            ag_arrival(l, k).wait_recv()
            go(ag_relay(l, k))
        await_gu(l, 0)
        gate_up(l, 0, c)
        relay_gu(l, 1, RELAYS[0] + RELAYS[1])
        for k in (1, 3, 5, 7):
            ag_arrival(l, k).wait_recv()
        gate_up(l, 0, 1 - c)
        relay_gu(l, 1, RELAYS[2] + RELAYS[3])
        finish_wd(l)
        await_gu(l, 1)
        gate_up(l, 1, 1 - c)
        for copy in sends:
            copy.wait_send()
        sends = []

        def send(copy):
            copy.start()
            sends.append(copy)

        for half in range(2):
            down(l, 1 - c, half)
            send(rs_core(l, half))
        gate_up(l, 1, c)
        for half in range(2):
            down(l, c, half)
            cols = (A, B)[half]
            rs_core(l, half).wait_recv()
            part[c, :, cols] = part[c, :, cols] + r1[l, :, cols]
            for t in range(2):
                send((rs_a, rs_b)[half](l, t))
        for t in range(2):
            rs_a(l, t).wait_recv()
            part[c, chip_rows(t, x), A] = part[c, chip_rows(t, x), A] + r2a[l, t]
        send(rs_a_last(l))
        for t in range(2):
            rs_b(l, t).wait_recv()
            part[c, chip_rows(y, t), B] = part[c, chip_rows(y, t), B] + r2b[l, t]
        send(rs_b_last(l))
        if l + 1 < LAYERS:
            relay_attn(l + 1)
            send_gu(l + 1, 0, GU_EARLY + GU_LATE)
        out = y_ref if l + 1 == LAYERS else res
        rs_a_last(l).wait_recv()
        out[:, A] = (mid[:, A].astype(F32) + (part[c, chip_rows(y, x), A] + r3a[l])).astype(BF)
        rs_b_last(l).wait_recv()
        out[:, B] = (mid[:, B].astype(F32) + (part[c, chip_rows(y, x), B] + r3b[l])).astype(BF)
        if l + 1 < LAYERS:
            start_layer(l + 1)
    for copy in sends + started:
        copy.wait_send()


def solution(mesh):
    vmem = pl.BlockSpec(memory_space=pltpu.VMEM)
    hbm = pl.BlockSpec(memory_space=pl.ANY)
    dma = pltpu.SemaphoreType.DMA
    inv_freq = ROPE_THETA ** -(np.arange(HEAD_DIM // 2) * 2.0 / HEAD_DIM)
    angles = np.tile(np.arange(SEQ)[:, None] * inv_freq[None, :].astype(np.float32), (2, 1)).astype(np.float32)
    cos_table = np.concatenate([np.cos(angles), np.cos(angles)], axis=1)
    sin_table = np.concatenate([-np.sin(angles), np.sin(angles)], axis=1)

    def local_forward(hidden, attn_norm, w_q, w_k, w_v, w_o, mlp_norm, w_gate, w_up, w_down):
        heads = []
        for g in range(KV_HEADS):
            heads += [w_q[:, :, GROUP * g : GROUP * (g + 1)], w_k[:, :, g : g + 1], w_v[:, :, g : g + 1]]
        wqkv = jnp.concatenate(heads, axis=2).reshape(LAYERS, ROWS, KV_HEADS * GROUP_COLS)
        y = pl.pallas_call(
            kernel,
            out_shape=jax.ShapeDtypeStruct((SEQ, DIM), BF),
            in_specs=[vmem] * 5 + [hbm] * 5,
            out_specs=vmem,
            scratch_shapes=[
                pltpu.VMEM((8, 2 * ROWS), F32),
                pltpu.VMEM((8, 8, 2 * ROWS), F32),
                pltpu.VMEM((8, DIM), F32),
                pltpu.VMEM((LAYERS, DIM, GROUP_COLS), BF),
                pltpu.VMEM((LAYERS, DIM, OUT_COLS), BF),
                pltpu.VMEM((LAYERS, 2, DIM, WINDOW), BF),
                pltpu.VMEM((LAYERS, WINDOW, DIM), BF),
                pltpu.VMEM((LAYERS, 2, EDGE, DIM), BF),
                pltpu.VMEM((SEQ, DIM), BF),
                pltpu.VMEM((SEQ, DIM), BF),
                pltpu.VMEM((LAYERS, 2 * SEQ, DIM), BF),
                pltpu.VMEM((2, GROUP * SEQ, HEAD_DIM), BF),
                pltpu.VMEM((2 * SEQ, HEAD_DIM), BF),
                pltpu.VMEM((2 * SEQ, HEAD_DIM), BF),
                pltpu.VMEM((LAYERS, 2 * SEQ, DIM), BF),
                pltpu.VMEM((LAYERS, 2 * SEQ, OUT_COLS), F32),
                pltpu.VMEM((LAYERS, SEQ, OUT_COLS), F32),
                pltpu.VMEM((LAYERS, 8 * SEQ, DIM), BF),
                pltpu.VMEM((8 * SEQ, WINDOW), BF),
                pltpu.VMEM((2, 4 * SEQ, DIM), F32),
                pltpu.VMEM((LAYERS, 4 * SEQ, DIM), F32),
                pltpu.VMEM((LAYERS, 2, SEQ, DIM // 2), F32),
                pltpu.VMEM((LAYERS, 2, SEQ, DIM // 2), F32),
                pltpu.VMEM((LAYERS, SEQ, DIM // 2), F32),
                pltpu.VMEM((LAYERS, SEQ, DIM // 2), F32),
                dma((7,)), dma((7,)),
                dma((LAYERS, 2, 2)), dma((LAYERS, 2, 2)),
                dma((LAYERS, 2, 2)), dma((LAYERS, 2, 2)),
                dma((LAYERS, 2, 5)), dma((LAYERS, 2, 5)),
                dma((LAYERS, 3)), dma((LAYERS, 3)),
                dma((LAYERS, 2, 2, 7)), dma((LAYERS, 2, 2, 7)),
                dma((LAYERS, 2, 2, 6)), dma((LAYERS, 2, 2, 6)),
                dma((LAYERS,)), dma((LAYERS,)),
                dma((LAYERS, 7)), dma((LAYERS, 7)),
                dma((LAYERS, 8)), dma((LAYERS, 8)),
                dma((LAYERS, 2)), dma((LAYERS, 2)), dma((LAYERS, 2)),
            ],
            compiler_params=pltpu.CompilerParams(collective_id=0, has_side_effects=True, vmem_limit_bytes=67043328),
        )(hidden.reshape(SEQ, DIM), attn_norm, mlp_norm, jnp.asarray(cos_table), jnp.asarray(sin_table), wqkv, w_o, w_gate, w_up, w_down)
        return y.reshape(1, SEQ, DIM)

    batch_spec = P(("dp", "fsdp"), None, None)
    gain_spec = P(None, "fsdp")
    proj_spec = P(None, "fsdp", None, None)
    mat_spec = P(None, "fsdp", None)
    return jax.shard_map(local_forward, mesh=mesh, in_specs=(batch_spec, gain_spec, proj_spec, proj_spec, proj_spec, mat_spec, gain_spec, mat_spec, mat_spec, mat_spec), out_specs=batch_spec, check_vma=False)
```

time: 273 us -> 215 us (0.79)
  Pallas kernels: 264 us -> 208 us
  other arithmetic: 4.06 us -> 0 us
    pallas_call x1, Pallas kernels: 264 us -> 208 us  [local_forward(): pl.pallas_call(kernel, out_shape=jax.ShapeDtypeStruct((SEQ, DIM), BF), in...]
where the time goes in v3:
time: 215 us; the launch traced here: 214 us
  Pallas kernels  208 us (97%)
  local copies, waits for them, and re-layouts  6.06 us (3%)
    pallas_call x1, Pallas kernels, local_forward(): pl.pallas_call(kernel, out_shape=jax.ShapeDtypeStruct((SEQ, DIM), BF), in...  208 us

profile of v3, /device:TPU:0, one launch (start us, length us, event | category | flops | bytes accessed | tf_op | source)
XLA Modules:
  0.0 214.4 jit_solution(12204124976372318198)
XLA Ops:
  0.0 0.0 copy-start
  0.0 0.0 copy-start.1
  0.0 1.5 fusion.1
  1.5 1.1 slice_dynamic-update-slice_fusion.1
  2.6 0.0 copy-done.1
  2.6 0.3 fusion
  2.9 0.0 copy-done
  3.0 0.1 slice_dynamic-update-slice_fusion
  3.1 1.4 copy_bitcast_fusion.wqkv_ref
  4.5 208.2 %shard_map.118 = bf16[64,1536]{1,0:T(8,128)(2,1)} custom-call(bf16[64,1536]{1,0:T(8,128)(2,1)} %bitcast.8, bf16[2,192]{1,0:T(2,128)(2,1)} %an_ref.1, bf16[2,192]{1,0:T(2,128)(2,1)} %mn_ref.1, f32[128,128]{1,0:T(8,128)} %constant.4.clone.cos_ref, f32[128,128]{1,0:T(8,128)} %constant.5.clone.sin_ref, bf16[2,192,2048]{2,1,0:T(8,128)(2,1)} %copy_bitcast_fusion.wqkv_ref, ...), custom_call_target="tpu_custom_call" | custom-call | tf_op jit(solution)/shard_map/pallas_call | solution.py:494
  212.7 1.6 copy.30
  (4 shorter events, 0.1 us)
Async XLA Ops:
  0.0 2.9 %copy-start = (bf16[2,192,12,128]{3,1,2,0:T(8,128)(2,1)S(1)}, bf16[2,192,12,128]{3,1,2,0:T(8,128)(2,1)}, u32[]{:S(2)}) copy-start(bf16[2,192,12,128]{3,1,2,0:T(8,128)(2,1)} %param.14) | copy-start | bytes 3538948
  0.0 2.6 %copy-start.1 = (bf16[2,192,2,128]{3,2,1,0:T(2,128)(2,1)S(1)}, bf16[2,192,2,128]{3,2,1,0:T(2,128)(2,1)}, u32[]{:S(2)}) copy-start(bf16[2,192,2,128]{3,2,1,0:T(2,128)(2,1)} %param.16) | copy-start | bytes 589828

commit v4 on v3

--- a/solution.py
+++ b/solution.py
@@ -27,16 +27,19 @@
 MAIN = 1088
 EDGE = 32
 HALF = ROWS // 2
-DIRECT = 112
-RELAY = ROWS - DIRECT
+DIRECT = ((96, 144), (96, 144))
 BF = jnp.bfloat16
 F32 = jnp.float32
 CHIPS = (2, 4, 6)
-PARTS = ((0, 768), (768, 384))
-GU_RELAYED = (2, 4, 6, 3, 5, 7)
+PARTS = ((0, 896), (896, 256))
+GU_RELAYED = (2, 4, 3, 5, 6, 7)
 RELAYS = (((2, 0), (4, 0)), ((2, 1), (4, 1)), ((6, 0), (6, 1), (3, 0), (5, 0)), ((3, 1), (5, 1), (7, 0), (7, 1)))
-GU_EARLY = ((2, 0), (4, 0))
-GU_LATE = ((2, 1), (4, 1), (6, 0), (6, 1), (3, 0), (5, 0), (3, 1), (5, 1), (7, 0), (7, 1), (1, 0), (1, 1))
+ONE = ((2, 0), (4, 0))
+TWO = ((2, 1), (4, 1))
+THREE = ((3, 0), (5, 0))
+FOUR = ((3, 1), (5, 1))
+FIVE = ((6, 0), (6, 1), (7, 0), (7, 1))
+CORE = ((1, 0), (1, 1))
 
 
 def aligned(value, size):
@@ -130,26 +133,22 @@
     def attn_core_own(l, m):
         return remote(attn_shard(l, m), attn_rows(l, m, 0), ac_s.at[l, m, 0], ac_r.at[l, m, 0], plane(1))
 
-    def send_attn(l):
-        for m in range(2):
-            for n in range(2):
-                go(attn_direct(l, m, n))
-        for m in range(2):
-            go(attn_core_own(l, m))
-            attn_own(l, m).start()
-
-    def relay_attn(l):
-        for m in range(2):
-            for n in range(2):
-                attn_arrival(l, m, n).wait_recv()
-                go(attn_turn(l, m, n))
-                go(attn_core(l, m, 1 + n, 2 + 2 * n))
-
-    def relay_attn_across(l):
-        for m in range(2):
-            for n in range(2):
-                attn_turn_arrival(l, m, n).wait_recv()
-                go(attn_core(l, m, 3 + n, 6, HALF * n, HALF))
+    def send_attn(l, m):
+        for n in range(2):
+            go(attn_direct(l, m, n))
+        go(attn_core_own(l, m))
+        attn_own(l, m).start()
+
+    def relay_attn(l, m):
+        for n in range(2):
+            attn_arrival(l, m, n).wait_recv()
+            go(attn_turn(l, m, n))
+            go(attn_core(l, m, 1 + n, 2 + 2 * n))
+
+    def relay_attn_across(l, m):
+        for n in range(2):
+            attn_turn_arrival(l, m, n).wait_recv()
+            go(attn_core(l, m, 3 + n, 6, HALF * n, HALF))
 
     def await_attn(l, m):
         attn_own(l, m).wait()
@@ -164,21 +163,21 @@
         return wgu.at[l, g, pl.ds(aligned(ROWS * peer(k) + start, 16), count), pl.ds(*PARTS[p])]
 
     def gu_direct(l, p, g, k):
-        start, count = (0, ROWS) if k == 1 else (aligned(RELAY * z, 16), DIRECT)
+        start, count = (0, ROWS) if k == 1 else (aligned((ROWS - DIRECT[l][p]) * z, 16), DIRECT[l][p])
         src = halves[g].at[l, pl.ds(start, count), pl.ds(aligned(window(peer(k)) + PARTS[p][0], 128), PARTS[p][1])]
         return remote(src, gu_rows(l, p, g, 0, start, count), gd_s.at[l, p, g, k - 1], gd_r.at[l, p, g, k - 1], plane(k))
 
     def gu_arrival(l, p, g, k):
-        start, count = (0, ROWS) if k == 1 else (RELAY * z, DIRECT)
+        start, count = (0, ROWS) if k == 1 else ((ROWS - DIRECT[l][p]) * z, DIRECT[l][p])
         dst = gu_rows(l, p, g, k, start, count)
         return remote(dst, dst, gd_s.at[l, p, g, k - 1], gd_r.at[l, p, g, k - 1], plane(k))
 
     def gu_across(l, p, g, k):
-        rows = gu_rows(l, p, g, k, DIRECT * z, RELAY)
+        rows = gu_rows(l, p, g, k, DIRECT[l][p] * z, ROWS - DIRECT[l][p])
         return remote(rows, rows, gz_s.at[l, p, g, k - 2], gz_r.at[l, p, g, k - 2], across)
 
     def gu_across_arrival(l, p, g, k):
-        dst = gu_rows(l, p, g, k, DIRECT * (1 - z), RELAY)
+        dst = gu_rows(l, p, g, k, DIRECT[l][p] * (1 - z), ROWS - DIRECT[l][p])
         return remote(dst, dst, gz_s.at[l, p, g, k - 2], gz_r.at[l, p, g, k - 2], across)
 
     def gu_own(l, g):
@@ -347,12 +346,14 @@
         if size % 256:
             columns(begin + size - 128, 128)
 
-    def down(l, b, half):
+    def down(l, p, b, half):
         rows = pl.ds(aligned(256 * b, 256), 256)
+        inner = pl.ds(*PARTS[p])
 
         def cols(n, carry):
             at = pl.ds(aligned(256 * n, 256), 256)
-            part[b, :, at] = jnp.dot(z_buf[rows, :], wd[l, :, at], preferred_element_type=F32)
+            add = jnp.dot(z_buf[rows, inner], wd[l, inner, at], preferred_element_type=F32)
+            part[b, :, at] = add if p == 0 else part[b, :, at] + add
             return carry
 
         lax.fori_loop(3 * half, 3 * half + 3, cols, 0)
@@ -379,82 +380,70 @@
     def rs_b_last(l):
         return remote(part.at[c, chip_rows(y, 1 - x), B], r3b.at[l], rs_s.at[l, 6], rs_r.at[l, 6], plane(2))
 
-    gain_mine[...] = jnp.zeros_like(gain_mine)
-    gain_mine[0:LAYERS, 0:ROWS] = an_ref[...].astype(F32)
-    gain_mine[LAYERS : 2 * LAYERS, 0:ROWS] = mn_ref[...].astype(F32)
-    gain_mine[...] = jnp.where(c == 1, pltpu.roll(gain_mine[...], ROWS, 1), gain_mine[...])
-    for k in range(1, 8):
-        go(gain_copy(k))
-    send_attn(0)
-    send_gu(0, 0, GU_EARLY)
-    gains[me] = gain_mine[...]
-    res[...] = x_ref[...]
-    for k in range(1, 8):
-        gain_arrival(k).wait_recv()
-    for p in range(4):
-        gain_rows[:, 384 * p : 384 * (p + 1)] = gains[2 * p] + gains[2 * p + 1]
-    start_layer(0)
-    relay_attn(0)
-    send_gu(0, 0, GU_LATE)
-    for l in range(LAYERS):
-        start_own(l)
-
     sends = []
-    for l in range(LAYERS):
-        relay_gu(l, 0, RELAYS[0])
-        relay_attn_across(l)
+
+    def send(copy):
+        copy.start()
+        sends.append(copy)
+
+    def attention(l):
         await_attn(l, 0)
         swap_in_arrival(l).wait_recv()
         project(l)
         attend(l)
         go(swap_heads(l))
-        relay_gu(l, 0, RELAYS[1])
+
+    def attention_out(l):
         await_attn(l, 1)
         swap_heads_arrival(l).wait_recv()
         project_out(l)
         go(swap_out(l))
-        relay_gu(l, 0, RELAYS[2])
+
+    def attention_end(l):
         swap_out(l).wait_recv()
         finish_attn(l)
         u_buf[l, pl.ds(aligned(SEQ * block(0), SEQ), SEQ), :] = normed(mid, 2 + l)
         for k in (2, 4, 6, 1):
             go(ag_copy(l, k))
-        send_gu(l, 1, GU_EARLY + GU_LATE)
-        if l + 1 < LAYERS:
-            send_attn(l + 1)
-        relay_gu(l, 0, RELAYS[3])
+        send_gu(l, 1, ONE + TWO + THREE + FOUR + FIVE + CORE)
+
+    def mlp(l, relays):
+        relay_gu(l, 0, relays)
         for k in CHIPS:
             ag_arrival(l, k).wait_recv()
             go(ag_relay(l, k))
         await_gu(l, 0)
         gate_up(l, 0, c)
-        relay_gu(l, 1, RELAYS[0] + RELAYS[1])
+        relay_gu(l, 1, ONE + TWO)
         for k in (1, 3, 5, 7):
             ag_arrival(l, k).wait_recv()
         gate_up(l, 0, 1 - c)
-        relay_gu(l, 1, RELAYS[2] + RELAYS[3])
+        relay_gu(l, 1, THREE + FOUR)
+        while sends:
+            sends.pop().wait_send()
         finish_wd(l)
+        for half in range(2):
+            down(l, 0, 1 - c, half)
+        relay_gu(l, 1, FIVE)
+        for half in range(2):
+            down(l, 0, c, half)
         await_gu(l, 1)
         gate_up(l, 1, 1 - c)
-        for copy in sends:
-            copy.wait_send()
-        sends = []
-
-        def send(copy):
-            copy.start()
-            sends.append(copy)
-
         for half in range(2):
-            down(l, 1 - c, half)
+            down(l, 1, 1 - c, half)
             send(rs_core(l, half))
+
+    def mlp_own(l):
         gate_up(l, 1, c)
         for half in range(2):
-            down(l, c, half)
+            down(l, 1, c, half)
             cols = (A, B)[half]
             rs_core(l, half).wait_recv()
             part[c, :, cols] = part[c, :, cols] + r1[l, :, cols]
             for t in range(2):
                 send((rs_a, rs_b)[half](l, t))
+
+    def rs_middle(l):
         for t in range(2):
             rs_a(l, t).wait_recv()
             part[c, chip_rows(t, x), A] = part[c, chip_rows(t, x), A] + r2a[l, t]
@@ -463,16 +452,69 @@
             rs_b(l, t).wait_recv()
             part[c, chip_rows(y, t), B] = part[c, chip_rows(y, t), B] + r2b[l, t]
         send(rs_b_last(l))
-        if l + 1 < LAYERS:
-            relay_attn(l + 1)
-            send_gu(l + 1, 0, GU_EARLY + GU_LATE)
-        out = y_ref if l + 1 == LAYERS else res
+
+    def rs_end(l, out):
         rs_a_last(l).wait_recv()
         out[:, A] = (mid[:, A].astype(F32) + (part[c, chip_rows(y, x), A] + r3a[l])).astype(BF)
         rs_b_last(l).wait_recv()
         out[:, B] = (mid[:, B].astype(F32) + (part[c, chip_rows(y, x), B] + r3b[l])).astype(BF)
-        if l + 1 < LAYERS:
-            start_layer(l + 1)
+
+    gain_mine[...] = jnp.zeros_like(gain_mine)
+    gain_mine[0:LAYERS, 0:ROWS] = an_ref[...].astype(F32)
+    gain_mine[LAYERS : 2 * LAYERS, 0:ROWS] = mn_ref[...].astype(F32)
+    gain_mine[...] = jnp.where(c == 1, pltpu.roll(gain_mine[...], ROWS, 1), gain_mine[...])
+    for k in range(1, 8):
+        go(gain_copy(k))
+    send_gu(0, 0, ONE + TWO)
+    send_attn(0, 0)
+    send_attn(0, 1)
+    gains[me] = gain_mine[...]
+    res[...] = x_ref[...]
+    for k in range(1, 8):
+        gain_arrival(k).wait_recv()
+    for p in range(4):
+        gain_rows[:, 384 * p : 384 * (p + 1)] = gains[2 * p] + gains[2 * p + 1]
+    start_layer(0)
+    relay_gu(0, 0, ONE + TWO)
+    relay_attn(0, 0)
+    relay_attn(0, 1)
+    send_gu(0, 0, THREE + FOUR + FIVE + CORE)
+    for l in range(LAYERS):
+        start_own(l)
+    relay_attn_across(0, 0)
+    attention(0)
+    relay_attn_across(0, 1)
+    relay_gu(0, 0, THREE)
+    attention_out(0)
+    relay_gu(0, 0, FOUR)
+    attention_end(0)
+    send_gu(1, 0, ONE)
+    send_attn(1, 0)
+    send_gu(1, 0, TWO)
+    mlp(0, FIVE)
+    relay_gu(1, 0, ONE)
+    mlp_own(0)
+    relay_gu(1, 0, TWO)
+    relay_attn(1, 0)
+    rs_middle(0)
+    send_gu(1, 0, THREE + FOUR)
+    send_attn(1, 1)
+    relay_attn_across(1, 0)
+    rs_end(0, res)
+    start_layer(1)
+    relay_gu(1, 0, THREE)
+    attention(1)
+    relay_gu(1, 0, FOUR)
+    relay_attn(1, 1)
+    send_gu(1, 0, FIVE + CORE)
+    relay_attn_across(1, 1)
+    attention_out(1)
+    relay_gu(1, 0, FIVE[:2])
+    attention_end(1)
+    mlp(1, FIVE[2:])
+    mlp_own(1)
+    rs_middle(1)
+    rs_end(1, y_ref)
     for copy in sends + started:
         copy.wait_send()
 

time: 215 us -> 203 us (0.944)
  Pallas kernels: 208 us -> 197 us
    pallas_call x1, Pallas kernels: 208 us -> 197 us  [local_forward(): pl.pallas_call(kernel, out_shape=jax.ShapeDtypeStruct((SEQ, DIM), BF), in...]
where the time goes in v4:
time: 203 us
  Pallas kernels  197 us (97%)
  local copies, waits for them, and re-layouts  6.06 us (3%)
    pallas_call x1, Pallas kernels, local_forward(): pl.pallas_call(kernel, out_shape=jax.ShapeDtypeStruct((SEQ, DIM), BF), in...  197 us

profile of v4, /device:TPU:0, one launch (start us, length us, event | category | flops | bytes accessed | tf_op | source)
XLA Modules:
  0.0 202.7 jit_solution(998287321275597626)
XLA Ops:
  0.0 0.0 copy-start
  0.0 0.0 copy-start.1
  0.0 1.5 fusion.1
  1.5 1.1 slice_dynamic-update-slice_fusion.1
  2.6 0.0 copy-done.1
  2.6 0.3 fusion
  2.9 0.0 copy-done
  3.0 0.1 slice_dynamic-update-slice_fusion
  3.1 1.4 copy_bitcast_fusion.wqkv_ref
  4.5 196.6 %shard_map.118 = bf16[64,1536]{1,0:T(8,128)(2,1)} custom-call(bf16[64,1536]{1,0:T(8,128)(2,1)} %bitcast.8, bf16[2,192]{1,0:T(2,128)(2,1)} %an_ref.1, bf16[2,192]{1,0:T(2,128)(2,1)} %mn_ref.1, f32[128,128]{1,0:T(8,128)} %constant.4.clone.cos_ref, f32[128,128]{1,0:T(8,128)} %constant.5.clone.sin_ref, bf16[2,192,2048]{2,1,0:T(8,128)(2,1)} %copy_bitcast_fusion.wqkv_ref, ...), custom_call_target="tpu_custom_call" | custom-call | tf_op jit(solution)/shard_map/pallas_call | solution.py:536
  201.1 1.6 copy.30
  (4 shorter events, 0.1 us)
Async XLA Ops:
  0.0 2.9 %copy-start = (bf16[2,192,12,128]{3,1,2,0:T(8,128)(2,1)S(1)}, bf16[2,192,12,128]{3,1,2,0:T(8,128)(2,1)}, u32[]{:S(2)}) copy-start(bf16[2,192,12,128]{3,1,2,0:T(8,128)(2,1)} %param.14) | copy-start | bytes 3538948
  0.0 2.6 %copy-start.1 = (bf16[2,192,2,128]{3,2,1,0:T(2,128)(2,1)S(1)}, bf16[2,192,2,128]{3,2,1,0:T(2,128)(2,1)}, u32[]{:S(2)}) copy-start(bf16[2,192,2,128]{3,2,1,0:T(2,128)(2,1)} %param.16) | copy-start | bytes 589828

commit v5 on v4

--- a/solution.py
+++ b/solution.py
@@ -17,8 +17,9 @@
 HEADS = 12
 KV_HEADS = 2
 HEAD_DIM = 128
+LANES = 128
+TILE = 256
 GROUP = HEADS // KV_HEADS
-GROUP_COLS = (GROUP + 2) * HEAD_DIM
 OUT_COLS = DIM // 2
 FFN = 8960
 ROWS = DIM // 8
@@ -27,27 +28,24 @@
 MAIN = 1088
 EDGE = 32
 HALF = ROWS // 2
-DIRECT = ((96, 144), (96, 144))
+DIRECT = ((96, 128), (96, 128))
 BF = jnp.bfloat16
 F32 = jnp.float32
-CHIPS = (2, 4, 6)
-PARTS = ((0, 896), (896, 256))
+PARTS = ((0, 768), (768, 384))
 GU_RELAYED = (2, 4, 3, 5, 6, 7)
 RELAYS = (((2, 0), (4, 0)), ((2, 1), (4, 1)), ((6, 0), (6, 1), (3, 0), (5, 0)), ((3, 1), (5, 1), (7, 0), (7, 1)))
-ONE = ((2, 0), (4, 0))
-TWO = ((2, 1), (4, 1))
-THREE = ((3, 0), (5, 0))
-FOUR = ((3, 1), (5, 1))
-FIVE = ((6, 0), (6, 1), (7, 0), (7, 1))
+ONE, TWO, THREE, FOUR = [tuple((k, g) for k in pair) for pair in ((2, 4), (3, 5)) for g in (0, 1)]
+FIVE = tuple((k, g) for k in (6, 7) for g in (0, 1))
 CORE = ((1, 0), (1, 1))
+KINDS = ((2, 0), (1,))
 
 
 def aligned(value, size):
     return pl.multiple_of(value, size)
 
 
-def kernel(x_ref, an_ref, mn_ref, cos_ref, sin_ref, wqkv_ref, wo_ref, wg_ref, wu_ref, wd_ref, y_ref,
-           gain_mine, gains, gain_rows, wq, wo, wgu, wd, edge, res, mid, n_buf, q_buf, k_buf, v_buf, o_buf, add_mine, add_got, u_buf, z_buf, part,
+def kernel(x_ref, an_ref, mn_ref, cos_ref, sin_ref, wq_ref, wo_ref, wkv_ref, wg_ref, wu_ref, wd_ref, y_ref,
+           gain_mine, gains, gain_rows, wq, wo, wkv, wgu, wd, edge, res, mid, n_buf, q_buf, k_buf, v_buf, o_buf, add_mine, add_got, u_buf, z_buf, part,
            r1, r2a, r2b, r3a, r3b,
            gain_s, gain_r, ad_s, ad_r, ax_s, ax_r, ac_s, ac_r, zx_s, zx_r, gd_s, gd_r, gz_s, gz_r, ed_s, ed_r, ag_s, ag_r, rs_s, rs_r,
            own_a, own_gu, own_wd):
@@ -57,20 +55,20 @@
     x = (me // 2) % 2
     y = me // 4
 
+    def place(k):
+        flips = (k % 2, (k // 2) % 2, k // 4)
+        return [1 - own if flip else own for own, flip in zip((c, x, y), flips)]
+
     def peer(k):
-        cc = 1 - c if k % 2 else c
-        xx = 1 - x if (k // 2) % 2 else x
-        yy = 1 - y if k // 4 else y
+        cc, xx, yy = place(k)
         return 4 * yy + 2 * xx + cc
 
     def block(k):
-        cc = 1 - c if k % 2 else c
-        xx = 1 - x if (k // 2) % 2 else x
-        yy = 1 - y if k // 4 else y
+        cc, xx, yy = place(k)
         return 4 * cc + 2 * yy + xx
 
     def window(j):
-        return aligned(128 * (35 * (j // 4) + 9 * (j % 4) - (j % 4) // 2), 128)
+        return aligned(LANES * (35 * (j // 4) + 9 * (j % 4) - (j % 4) // 2), LANES)
 
     def plane(k):
         return (z, peer(k))
@@ -98,15 +96,18 @@
         dst = gains.at[peer(k)]
         return remote(dst, dst, gain_s.at[k - 1], gain_r.at[k - 1], plane(k))
 
-    attn_src = (wqkv_ref, wo_ref)
-    attn_dst = (wq, wo)
-    attn_cols = (GROUP_COLS, OUT_COLS)
+    attn_src = (wq_ref, wo_ref, wkv_ref)
+    attn_dst = (wq, wo, wkv)
+    share = (GROUP, OUT_COLS, KV_HEADS)
 
     def attn_rows(l, m, k, start=0, count=ROWS):
-        return attn_dst[m].at[l, pl.ds(aligned(ROWS * peer(k) + start, 32), count), :]
+        rows = pl.ds(aligned(ROWS * peer(k) + start, 32), count)
+        return attn_dst[m].at[l, rows, :] if m == 1 else attn_dst[m].at[l, :, rows, :]
 
     def attn_shard(l, m):
-        return attn_src[m].at[l, :, pl.ds(aligned(attn_cols[m] * z, 128), attn_cols[m])]
+        if m == 1:
+            return attn_src[m].at[l, :, pl.ds(aligned(share[m] * z, LANES), share[m])]
+        return attn_src[m].at[l, pl.ds(share[m] * z, share[m]), :, :]
 
     def attn_own(l, m):
         return pltpu.make_async_copy(attn_shard(l, m), attn_rows(l, m, 0), own_a.at[l, m])
@@ -133,29 +134,33 @@
     def attn_core_own(l, m):
         return remote(attn_shard(l, m), attn_rows(l, m, 0), ac_s.at[l, m, 0], ac_r.at[l, m, 0], plane(1))
 
-    def send_attn(l, m):
-        for n in range(2):
-            go(attn_direct(l, m, n))
-        go(attn_core_own(l, m))
-        attn_own(l, m).start()
-
-    def relay_attn(l, m):
-        for n in range(2):
-            attn_arrival(l, m, n).wait_recv()
-            go(attn_turn(l, m, n))
-            go(attn_core(l, m, 1 + n, 2 + 2 * n))
-
-    def relay_attn_across(l, m):
-        for n in range(2):
-            attn_turn_arrival(l, m, n).wait_recv()
-            go(attn_core(l, m, 3 + n, 6, HALF * n, HALF))
-
-    def await_attn(l, m):
-        attn_own(l, m).wait()
-        attn_core(l, m, 0, 1).wait_recv()
-        for n in range(2):
-            attn_core(l, m, 1 + n, 3 + 2 * n).wait_recv()
-            attn_core(l, m, 3 + n, 7, HALF * n, HALF).wait_recv()
+    def send_attn(l, out):
+        for m in KINDS[out]:
+            for n in range(2):
+                go(attn_direct(l, m, n))
+            go(attn_core_own(l, m))
+            attn_own(l, m).start()
+
+    def relay_attn(l, out):
+        for m in KINDS[out]:
+            for n in range(2):
+                attn_arrival(l, m, n).wait_recv()
+                go(attn_turn(l, m, n))
+                go(attn_core(l, m, 1 + n, 2 + 2 * n))
+
+    def relay_attn_across(l, out):
+        for m in KINDS[out]:
+            for n in range(2):
+                attn_turn_arrival(l, m, n).wait_recv()
+                go(attn_core(l, m, 3 + n, 6, HALF * n, HALF))
+
+    def await_attn(l, out):
+        for m in KINDS[out]:
+            attn_own(l, m).wait()
+            attn_core(l, m, 0, 1).wait_recv()
+            for n in range(2):
+                attn_core(l, m, 1 + n, 3 + 2 * n).wait_recv()
+                attn_core(l, m, 3 + n, 7, HALF * n, HALF).wait_recv()
 
     halves = (wg_ref, wu_ref)
 
@@ -164,7 +169,7 @@
 
     def gu_direct(l, p, g, k):
         start, count = (0, ROWS) if k == 1 else (aligned((ROWS - DIRECT[l][p]) * z, 16), DIRECT[l][p])
-        src = halves[g].at[l, pl.ds(start, count), pl.ds(aligned(window(peer(k)) + PARTS[p][0], 128), PARTS[p][1])]
+        src = halves[g].at[l, pl.ds(start, count), pl.ds(aligned(window(peer(k)) + PARTS[p][0], LANES), PARTS[p][1])]
         return remote(src, gu_rows(l, p, g, 0, start, count), gd_s.at[l, p, g, k - 1], gd_r.at[l, p, g, k - 1], plane(k))
 
     def gu_arrival(l, p, g, k):
@@ -226,9 +231,9 @@
         edge_core(l).wait_recv()
         own, got = edge[l, 0], edge[l, 1]
         none = jnp.zeros_like(own)
-        place = MAIN * (1 - x)
-        wd[l, pl.ds(aligned(place, EDGE), EDGE), :] = jnp.where(takes, jnp.where(x == 0, own, got), none)
-        wd[l, pl.ds(aligned(place + EDGE, EDGE), EDGE), :] = jnp.where(takes, jnp.where(x == 0, got, own), none)
+        edge_row = MAIN * (1 - x)
+        wd[l, pl.ds(aligned(edge_row, EDGE), EDGE), :] = jnp.where(takes, jnp.where(x == 0, own, got), none)
+        wd[l, pl.ds(aligned(edge_row + EDGE, EDGE), EDGE), :] = jnp.where(takes, jnp.where(x == 0, got, own), none)
 
     first = jnp.where(takes, 0, 2 * EDGE * x)
     last = jnp.where(takes, WINDOW, 2 * EDGE * x + MAIN)
@@ -239,7 +244,7 @@
         return (wide * inv_rms * gain_rows[row : row + 1, :]).astype(BF)
 
     mine, other = pl.ds(aligned(SEQ * z, SEQ), SEQ), pl.ds(aligned(SEQ * (1 - z), SEQ), SEQ)
-    left, right = pl.ds(aligned(OUT_COLS * z, 128), OUT_COLS), pl.ds(aligned(OUT_COLS * (1 - z), 128), OUT_COLS)
+    left, right = pl.ds(aligned(OUT_COLS * z, LANES), OUT_COLS), pl.ds(aligned(OUT_COLS * (1 - z), LANES), OUT_COLS)
 
     def swap_in(l):
         rows = n_buf.at[l, mine, :]
@@ -271,20 +276,21 @@
             return (v * cos + pltpu.roll(v, HEAD_DIM // 2, 1) * sin).astype(BF)
 
         def two_heads(n):
-            return jnp.dot(n_buf[l], wq[l, :, pl.ds(aligned(256 * n, 256), 256)], preferred_element_type=F32)
+            pair = (wkv[l, 0], wkv[l, 1]) if n is None else (wq[l, 2 * n], wq[l, 2 * n + 1])
+            return jnp.dot(n_buf[l], jnp.concatenate(pair, axis=1), preferred_element_type=F32)
 
         def q_heads(n, carry):
             pair = two_heads(n)
             for t in range(2):
-                turned = rotate(pair[:, 128 * t : 128 * (t + 1)])
+                turned = rotate(pair[:, LANES * t : LANES * (t + 1)])
                 for seq in range(2):
                     q_buf[seq, pl.ds(aligned((2 * n + t) * SEQ, SEQ), SEQ), :] = turned[SEQ * seq : SEQ * (seq + 1)]
             return carry
 
         lax.fori_loop(0, GROUP // 2, q_heads, 0)
-        pair = two_heads(GROUP // 2)
-        k_buf[...] = rotate(pair[:, :128])
-        v_buf[...] = pair[:, 128:].astype(BF)
+        pair = two_heads(None)
+        k_buf[...] = rotate(pair[:, :LANES])
+        v_buf[...] = pair[:, LANES:].astype(BF)
 
     def attend(l):
         row = lax.broadcasted_iota(jnp.int32, (GROUP * SEQ, SEQ), 0) % SEQ
@@ -297,61 +303,81 @@
             probs = (e / jnp.sum(e, axis=-1, keepdims=True)).astype(BF)
             o = jnp.dot(probs, v_buf[rows, :], preferred_element_type=F32).astype(BF)
             for j in range(GROUP):
-                o_buf[l, rows, pl.ds(aligned(OUT_COLS * z + HEAD_DIM * j, 128), HEAD_DIM)] = o[j * SEQ : (j + 1) * SEQ]
+                o_buf[l, rows, pl.ds(aligned(OUT_COLS * z + HEAD_DIM * j, LANES), HEAD_DIM)] = o[j * SEQ : (j + 1) * SEQ]
 
     def project_out(l):
         def out_cols(n, carry):
-            cols = pl.ds(aligned(256 * n, 256), 256)
+            cols = pl.ds(aligned(TILE * n, TILE), TILE)
             add_mine[l, :, cols] = jnp.dot(o_buf[l], wo[l, :, cols], preferred_element_type=F32)
             return carry
 
-        lax.fori_loop(0, OUT_COLS // 256, out_cols, 0)
+        lax.fori_loop(0, OUT_COLS // TILE, out_cols, 0)
 
     def finish_attn(l):
         mid[:, left] = (res[:, left].astype(F32) + add_mine[l, mine, :]).astype(BF)
         mid[:, right] = (res[:, right].astype(F32) + add_got[l]).astype(BF)
 
-    def seq_rows(l, k):
-        return u_buf.at[l, pl.ds(aligned(SEQ * block(k), SEQ), SEQ), :]
-
-    def ag_copy(l, k):
-        return remote(seq_rows(l, 0), seq_rows(l, 0), ag_s.at[l, k - 1], ag_r.at[l, k - 1], plane(k))
-
-    def ag_relay(l, k):
-        return remote(seq_rows(l, k), seq_rows(l, k), ag_s.at[l, k], ag_r.at[l, k], plane(1))
-
-    def ag_arrival(l, k):
-        dst = seq_rows(l, k)
-        return remote(dst, dst, ag_s.at[l, k - 1], ag_r.at[l, k - 1], plane(k))
+    def seq_rows(l, k, start=0, count=SEQ):
+        return u_buf.at[l, pl.ds(aligned(SEQ * block(k) + start, 32), count), :]
+
+    def ag(l, sem, k, to, *rows):
+        part_rows = seq_rows(l, k, *rows)
+        return remote(part_rows, part_rows, ag_s.at[l, sem], ag_r.at[l, sem], plane(to))
+
+    def ag_half(n):
+        return SEQ // 2 * n, SEQ // 2
+
+    def ag_start(l):
+        for n in range(2):
+            go(ag(l, n, 0, 2 + 2 * n))
+        go(ag(l, 2, 0, 1))
+
+    def ag_turn(l):
+        for n in range(2):
+            k = 2 + 2 * n
+            ag(l, n, k, k).wait_recv()
+            go(ag(l, 5 + n, k, 6 - k, *ag_half(n)))
+            go(ag(l, 3 + n, k, 1))
+
+    def ag_across(l):
+        for n in range(2):
+            ag(l, 5 + n, 6, 4 - 2 * n, *ag_half(n)).wait_recv()
+            go(ag(l, 7 + n, 6, 1, *ag_half(n)))
+
+    def ag_end(l):
+        ag(l, 2, 1, 1).wait_recv()
+        for n in range(2):
+            ag(l, 3 + n, 3 + 2 * n, 1).wait_recv()
+            ag(l, 7 + n, 7, 1, *ag_half(n)).wait_recv()
 
     def gate_up(l, p, b):
-        rows = pl.ds(aligned(256 * b, 256), 256)
+        rows = pl.ds(aligned(TILE * b, TILE), TILE)
         begin, size = PARTS[p]
 
         def columns(start, width):
-            at = pl.ds(aligned(start, 128), width)
+            at = pl.ds(aligned(start, LANES), width)
             u = u_buf[l, rows, :]
             gate = jnp.dot(u, wgu[l, 0, :, at], preferred_element_type=F32).astype(BF).astype(F32)
             up = jnp.dot(u, wgu[l, 1, :, at], preferred_element_type=F32).astype(BF).astype(F32)
             gated = (jax.nn.silu(gate) * up).astype(BF)
-            place = start + lax.broadcasted_iota(jnp.int32, (256, width), 1)
-            valid = (place >= first) & (place < last)
+            spot = start + lax.broadcasted_iota(jnp.int32, (TILE, width), 1)
+            valid = (spot >= first) & (spot < last)
             z_buf[rows, at] = jnp.where(valid, gated, jnp.zeros_like(gated))
 
         def cols(n, carry):
-            columns(begin + 256 * n, 256)
+            columns(begin + TILE * n, TILE)
             return carry
 
-        lax.fori_loop(0, size // 256, cols, 0)
-        if size % 256:
-            columns(begin + size - 128, 128)
+        lax.fori_loop(0, size // TILE, cols, 0)
+        if size % TILE:
+            columns(begin + size - LANES, LANES)
 
     def down(l, p, b, half):
-        rows = pl.ds(aligned(256 * b, 256), 256)
+        rows = pl.ds(aligned(TILE * b, TILE), TILE)
         inner = pl.ds(*PARTS[p])
 
         def cols(n, carry):
-            at = pl.ds(aligned(256 * n, 256), 256)
+            at = pl.ds(aligned(TILE * n, TILE), TILE)
             add = jnp.dot(z_buf[rows, inner], wd[l, inner, at], preferred_element_type=F32)
             part[b, :, at] = add if p == 0 else part[b, :, at] + add
             return carry
@@ -368,11 +394,11 @@
         sem = 7 if half else 0
         return remote(part.at[1 - c, :, cols], r1.at[l, :, cols], rs_s.at[l, sem], rs_r.at[l, sem], plane(1))
 
-    def rs_a(l, yy):
-        return remote(part.at[c, chip_rows(yy, 1 - x), A], r2a.at[l, yy], rs_s.at[l, 1 + yy], rs_r.at[l, 1 + yy], plane(2))
-
-    def rs_b(l, xx):
-        return remote(part.at[c, chip_rows(1 - y, xx), B], r2b.at[l, xx], rs_s.at[l, 3 + xx], rs_r.at[l, 3 + xx], plane(4))
+    def rs_a(l, t):
+        return remote(part.at[c, chip_rows((1 - y, y)[t], 1 - x), A], r2a.at[l, t], rs_s.at[l, 1 + t], rs_r.at[l, 1 + t], plane(2))
+
+    def rs_b(l, t):
+        return remote(part.at[c, chip_rows(1 - y, (1 - x, x)[t]), B], r2b.at[l, t], rs_s.at[l, 3 + t], rs_r.at[l, 3 + t], plane(4))
 
     def rs_a_last(l):
         return remote(part.at[c, chip_rows(1 - y, x), A], r3a.at[l], rs_s.at[l, 5], rs_r.at[l, 5], plane(4))
@@ -403,22 +429,25 @@
         swap_out(l).wait_recv()
         finish_attn(l)
         u_buf[l, pl.ds(aligned(SEQ * block(0), SEQ), SEQ), :] = normed(mid, 2 + l)
-        for k in (2, 4, 6, 1):
-            go(ag_copy(l, k))
-        send_gu(l, 1, ONE + TWO + THREE + FOUR + FIVE + CORE)
+        ag_start(l)
+        send_gu(l, 1, ONE + TWO)
 
     def mlp(l, relays):
         relay_gu(l, 0, relays)
-        for k in CHIPS:
-            ag_arrival(l, k).wait_recv()
-            go(ag_relay(l, k))
+        ag_turn(l)
+        send_gu(l, 1, THREE + FOUR + FIVE + CORE)
+        if l + 1 < LAYERS:
+            send_gu(l + 1, 0, ONE)
+            send_attn(l + 1, 0)
+            send_gu(l + 1, 0, TWO)
+        relay_gu(l, 1, ONE + TWO)
+        ag_across(l)
         await_gu(l, 0)
         gate_up(l, 0, c)
-        relay_gu(l, 1, ONE + TWO)
-        for k in (1, 3, 5, 7):
-            ag_arrival(l, k).wait_recv()
+        relay_gu(l, 1, THREE)
+        ag_end(l)
         gate_up(l, 0, 1 - c)
-        relay_gu(l, 1, THREE + FOUR)
+        relay_gu(l, 1, FOUR)
         while sends:
             sends.pop().wait_send()
         finish_wd(l)
@@ -443,15 +472,20 @@
             for t in range(2):
                 send((rs_a, rs_b)[half](l, t))
 
+    def rs_add(l, t):
+        row_a, row_b = chip_rows((1 - y, y)[t], x), chip_rows(y, (1 - x, x)[t])
+        rs_a(l, t).wait_recv()
+        part[c, row_a, A] = part[c, row_a, A] + r2a[l, t]
+        if t == 0:
+            send(rs_a_last(l))
+        rs_b(l, t).wait_recv()
+        part[c, row_b, B] = part[c, row_b, B] + r2b[l, t]
+        if t == 0:
+            send(rs_b_last(l))
+
     def rs_middle(l):
         for t in range(2):
-            rs_a(l, t).wait_recv()
-            part[c, chip_rows(t, x), A] = part[c, chip_rows(t, x), A] + r2a[l, t]
-        send(rs_a_last(l))
-        for t in range(2):
-            rs_b(l, t).wait_recv()
-            part[c, chip_rows(y, t), B] = part[c, chip_rows(y, t), B] + r2b[l, t]
-        send(rs_b_last(l))
+            rs_add(l, t)
 
     def rs_end(l, out):
         rs_a_last(l).wait_recv()
@@ -465,9 +499,9 @@
     gain_mine[...] = jnp.where(c == 1, pltpu.roll(gain_mine[...], ROWS, 1), gain_mine[...])
     for k in range(1, 8):
         go(gain_copy(k))
-    send_gu(0, 0, ONE + TWO)
-    send_attn(0, 0)
-    send_attn(0, 1)
+    send_gu(0, 0, ONE + TWO + THREE)
+    for m in range(2):
+        send_attn(0, m)
     gains[me] = gain_mine[...]
     res[...] = x_ref[...]
     for k in range(1, 8):
@@ -475,43 +509,38 @@
     for p in range(4):
         gain_rows[:, 384 * p : 384 * (p + 1)] = gains[2 * p] + gains[2 * p + 1]
     start_layer(0)
-    relay_gu(0, 0, ONE + TWO)
-    relay_attn(0, 0)
-    relay_attn(0, 1)
-    send_gu(0, 0, THREE + FOUR + FIVE + CORE)
+    relay_gu(0, 0, ONE + TWO + THREE)
+    for m in range(2):
+        relay_attn(0, m)
+    send_gu(0, 0, FOUR + FIVE + CORE)
     for l in range(LAYERS):
         start_own(l)
     relay_attn_across(0, 0)
     attention(0)
     relay_attn_across(0, 1)
-    relay_gu(0, 0, THREE)
     attention_out(0)
-    relay_gu(0, 0, FOUR)
+    relay_gu(0, 0, FOUR + FIVE[:2])
     attention_end(0)
-    send_gu(1, 0, ONE)
-    send_attn(1, 0)
-    send_gu(1, 0, TWO)
-    mlp(0, FIVE)
+    mlp(0, FIVE[2:])
     relay_gu(1, 0, ONE)
     mlp_own(0)
     relay_gu(1, 0, TWO)
     relay_attn(1, 0)
     rs_middle(0)
-    send_gu(1, 0, THREE + FOUR)
     send_attn(1, 1)
+    send_gu(1, 0, THREE)
     relay_attn_across(1, 0)
     rs_end(0, res)
     start_layer(1)
+    attention(1)
+    relay_attn(1, 1)
+    send_gu(1, 0, FOUR + FIVE + CORE)
     relay_gu(1, 0, THREE)
-    attention(1)
-    relay_gu(1, 0, FOUR)
-    relay_attn(1, 1)
-    send_gu(1, 0, FIVE + CORE)
     relay_attn_across(1, 1)
     attention_out(1)
-    relay_gu(1, 0, FIVE[:2])
+    relay_gu(1, 0, FOUR)
     attention_end(1)
-    mlp(1, FIVE[2:])
+    mlp(1, FIVE)
     mlp_own(1)
     rs_middle(1)
     rs_end(1, y_ref)
@@ -523,27 +552,27 @@
     vmem = pl.BlockSpec(memory_space=pltpu.VMEM)
     hbm = pl.BlockSpec(memory_space=pl.ANY)
     dma = pltpu.SemaphoreType.DMA
+    pairs = [(7,), (LAYERS, 3, 2), (LAYERS, 3, 2), (LAYERS, 3, 5), (LAYERS, 3), (LAYERS, 2, 2, 7), (LAYERS, 2, 2, 6), (LAYERS,), (LAYERS, 9), (LAYERS, 8)]
     inv_freq = ROPE_THETA ** -(np.arange(HEAD_DIM // 2) * 2.0 / HEAD_DIM)
     angles = np.tile(np.arange(SEQ)[:, None] * inv_freq[None, :].astype(np.float32), (2, 1)).astype(np.float32)
     cos_table = np.concatenate([np.cos(angles), np.cos(angles)], axis=1)
     sin_table = np.concatenate([-np.sin(angles), np.sin(angles)], axis=1)
 
     def local_forward(hidden, attn_norm, w_q, w_k, w_v, w_o, mlp_norm, w_gate, w_up, w_down):
-        heads = []
-        for g in range(KV_HEADS):
-            heads += [w_q[:, :, GROUP * g : GROUP * (g + 1)], w_k[:, :, g : g + 1], w_v[:, :, g : g + 1]]
-        wqkv = jnp.concatenate(heads, axis=2).reshape(LAYERS, ROWS, KV_HEADS * GROUP_COLS)
+        wq = w_q.transpose(0, 2, 1, 3)
+        wkv = jnp.stack([w_k, w_v], axis=3).reshape(LAYERS, ROWS, 2 * KV_HEADS, HEAD_DIM).transpose(0, 2, 1, 3)
         y = pl.pallas_call(
             kernel,
             out_shape=jax.ShapeDtypeStruct((SEQ, DIM), BF),
-            in_specs=[vmem] * 5 + [hbm] * 5,
+            in_specs=[vmem] * 5 + [hbm] * 6,
             out_specs=vmem,
             scratch_shapes=[
                 pltpu.VMEM((8, 2 * ROWS), F32),
                 pltpu.VMEM((8, 8, 2 * ROWS), F32),
                 pltpu.VMEM((8, DIM), F32),
-                pltpu.VMEM((LAYERS, DIM, GROUP_COLS), BF),
+                pltpu.VMEM((LAYERS, GROUP, DIM, HEAD_DIM), BF),
                 pltpu.VMEM((LAYERS, DIM, OUT_COLS), BF),
+                pltpu.VMEM((LAYERS, KV_HEADS, DIM, HEAD_DIM), BF),
                 pltpu.VMEM((LAYERS, 2, DIM, WINDOW), BF),
                 pltpu.VMEM((LAYERS, WINDOW, DIM), BF),
                 pltpu.VMEM((LAYERS, 2, EDGE, DIM), BF),
@@ -564,20 +593,9 @@
                 pltpu.VMEM((LAYERS, 2, SEQ, DIM // 2), F32),
                 pltpu.VMEM((LAYERS, SEQ, DIM // 2), F32),
                 pltpu.VMEM((LAYERS, SEQ, DIM // 2), F32),
-                dma((7,)), dma((7,)),
-                dma((LAYERS, 2, 2)), dma((LAYERS, 2, 2)),
-                dma((LAYERS, 2, 2)), dma((LAYERS, 2, 2)),
-                dma((LAYERS, 2, 5)), dma((LAYERS, 2, 5)),
-                dma((LAYERS, 3)), dma((LAYERS, 3)),
-                dma((LAYERS, 2, 2, 7)), dma((LAYERS, 2, 2, 7)),
-                dma((LAYERS, 2, 2, 6)), dma((LAYERS, 2, 2, 6)),
-                dma((LAYERS,)), dma((LAYERS,)),
-                dma((LAYERS, 7)), dma((LAYERS, 7)),
-                dma((LAYERS, 8)), dma((LAYERS, 8)),
-                dma((LAYERS, 2)), dma((LAYERS, 2)), dma((LAYERS, 2)),
-            ],
+            ] + [dma(shape) for shape in pairs for end in range(2)] + [dma((LAYERS, 3))] * 3,
             compiler_params=pltpu.CompilerParams(collective_id=0, has_side_effects=True, vmem_limit_bytes=67043328),
-        )(hidden.reshape(SEQ, DIM), attn_norm, mlp_norm, jnp.asarray(cos_table), jnp.asarray(sin_table), wqkv, w_o, w_gate, w_up, w_down)
+        )(hidden.reshape(SEQ, DIM), attn_norm, mlp_norm, jnp.asarray(cos_table), jnp.asarray(sin_table), wq, w_o, wkv, w_gate, w_up, w_down)
         return y.reshape(1, SEQ, DIM)
 
     batch_spec = P(("dp", "fsdp"), None, None)

time: 203 us -> 199 us (0.980)
  Pallas kernels: 197 us -> 193 us
  local copies, waits for them, and re-layouts: 6.06 us -> 2.41 us
    pallas_call x1, Pallas kernels: 197 us -> 193 us  [local_forward(): pl.pallas_call(kernel, out_shape=jax.ShapeDtypeStruct((SEQ, DIM), BF), in...]
where the time goes in v5:
time: 199 us; the launch traced here: 197 us
  Pallas kernels  193 us (97%)
  local copies, waits for them, and re-layouts  2.41 us (1%)
    pallas_call x1, Pallas kernels, local_forward(): pl.pallas_call(kernel, out_shape=jax.ShapeDtypeStruct((SEQ, DIM), BF), in...  193 us

profile of v5, /device:TPU:0, one launch (start us, length us, event | category | flops | bytes accessed | tf_op | source)
XLA Modules:
  0.0 197.5 jit_solution(9599036013362296664)
XLA Ops:
  0.0 1.6 pad_maximum_fusion
  1.6 0.8 copy.13
  2.4 193.4 %shard_map.118 = bf16[64,1536]{1,0:T(8,128)(2,1)} custom-call(bf16[64,1536]{1,0:T(8,128)(2,1)} %bitcast.11, bf16[2,192]{1,0:T(2,128)(2,1)} %an_ref.1, bf16[2,192]{1,0:T(2,128)(2,1)} %mn_ref.1, f32[128,128]{1,0:T(8,128)} %constant.4.clone.cos_ref, f32[128,128]{1,0:T(8,128)} %constant.5.clone.sin_ref, bf16[2,12,192,128]{3,2,1,0:T(8,128)(2,1)} %bitcast.9, ...), custom_call_target="tpu_custom_call" | custom-call | tf_op jit(solution)/shard_map/pallas_call | solution.py:564
  195.8 1.6 copy.15

commit v6 on v5

--- a/solution.py
+++ b/solution.py
@@ -30,6 +30,7 @@
 HALF = ROWS // 2
 DIRECT = ((96, 128), (96, 128))
 BF = jnp.bfloat16
+BOTH = range(2)
 F32 = jnp.float32
 PARTS = ((0, 768), (768, 384))
 GU_RELAYED = (2, 4, 3, 5, 6, 7)
@@ -37,14 +38,14 @@
 ONE, TWO, THREE, FOUR = [tuple((k, g) for k in pair) for pair in ((2, 4), (3, 5)) for g in (0, 1)]
 FIVE = tuple((k, g) for k in (6, 7) for g in (0, 1))
 CORE = ((1, 0), (1, 1))
-KINDS = ((2, 0), (1,))
+KINDS = ((2, 3, 0), (1,))
 
 
 def aligned(value, size):
     return pl.multiple_of(value, size)
 
 
-def kernel(x_ref, an_ref, mn_ref, cos_ref, sin_ref, wq_ref, wo_ref, wkv_ref, wg_ref, wu_ref, wd_ref, y_ref,
+def kernel(x_ref, an_ref, mn_ref, cos_ref, sin_ref, wq_ref, wo_ref, wk_ref, wv_ref, wg_ref, wu_ref, wd_ref, y_ref,
            gain_mine, gains, gain_rows, wq, wo, wkv, wgu, wd, edge, res, mid, n_buf, q_buf, k_buf, v_buf, o_buf, add_mine, add_got, u_buf, z_buf, part,
            r1, r2a, r2b, r3a, r3b,
            gain_s, gain_r, ad_s, ad_r, ax_s, ax_r, ac_s, ac_r, zx_s, zx_r, gd_s, gd_r, gz_s, gz_r, ed_s, ed_r, ag_s, ag_r, rs_s, rs_r,
@@ -96,13 +97,14 @@
         dst = gains.at[peer(k)]
         return remote(dst, dst, gain_s.at[k - 1], gain_r.at[k - 1], plane(k))
 
-    attn_src = (wq_ref, wo_ref, wkv_ref)
-    attn_dst = (wq, wo, wkv)
-    share = (GROUP, OUT_COLS, KV_HEADS)
+    attn_src = (wq_ref, wo_ref, wk_ref, wv_ref)
+    share = (GROUP, OUT_COLS, 1, 1)
+    attn_dst = (wq, wo, wkv, wkv)
+    heads_at = (pl.ds(0, GROUP), None, pl.ds(0, 1), pl.ds(1, 1))
 
     def attn_rows(l, m, k, start=0, count=ROWS):
         rows = pl.ds(aligned(ROWS * peer(k) + start, 32), count)
-        return attn_dst[m].at[l, rows, :] if m == 1 else attn_dst[m].at[l, :, rows, :]
+        return attn_dst[m].at[l, rows, :] if m == 1 else attn_dst[m].at[l, heads_at[m], rows, :]
 
     def attn_shard(l, m):
         if m == 1:
@@ -136,21 +138,21 @@
 
     def send_attn(l, out):
         for m in KINDS[out]:
-            for n in range(2):
+            for n in BOTH:
                 go(attn_direct(l, m, n))
             go(attn_core_own(l, m))
             attn_own(l, m).start()
 
     def relay_attn(l, out):
         for m in KINDS[out]:
-            for n in range(2):
+            for n in BOTH:
                 attn_arrival(l, m, n).wait_recv()
                 go(attn_turn(l, m, n))
                 go(attn_core(l, m, 1 + n, 2 + 2 * n))
 
     def relay_attn_across(l, out):
         for m in KINDS[out]:
-            for n in range(2):
+            for n in BOTH:
                 attn_turn_arrival(l, m, n).wait_recv()
                 go(attn_core(l, m, 3 + n, 6, HALF * n, HALF))
 
@@ -158,7 +160,7 @@
         for m in KINDS[out]:
             attn_own(l, m).wait()
             attn_core(l, m, 0, 1).wait_recv()
-            for n in range(2):
+            for n in BOTH:
                 attn_core(l, m, 1 + n, 3 + 2 * n).wait_recv()
                 attn_core(l, m, 3 + n, 7, HALF * n, HALF).wait_recv()
 
@@ -199,16 +201,16 @@
             go(gu_across(l, p, g, k))
 
     def await_gu(l, p):
-        for g in range(2):
+        for g in BOTH:
             gu_arrival(l, p, g, 1).wait_recv()
             if p == 0:
                 gu_own(l, g).wait()
         for k in GU_RELAYED:
-            for g in range(2):
+            for g in BOTH:
                 gu_across_arrival(l, p, g, k).wait_recv()
 
     def start_own(l):
-        for g in range(2):
+        for g in BOTH:
             gu_own(l, g).start()
         wd_copy(l).start()
         edge_own(l).start()
@@ -281,9 +283,9 @@
 
         def q_heads(n, carry):
             pair = two_heads(n)
-            for t in range(2):
+            for t in BOTH:
                 turned = rotate(pair[:, LANES * t : LANES * (t + 1)])
-                for seq in range(2):
+                for seq in BOTH:
                     q_buf[seq, pl.ds(aligned((2 * n + t) * SEQ, SEQ), SEQ), :] = turned[SEQ * seq : SEQ * (seq + 1)]
             return carry
 
@@ -295,7 +297,7 @@
     def attend(l):
         row = lax.broadcasted_iota(jnp.int32, (GROUP * SEQ, SEQ), 0) % SEQ
         col = lax.broadcasted_iota(jnp.int32, (GROUP * SEQ, SEQ), 1)
-        for seq in range(2):
+        for seq in BOTH:
             rows = slice(SEQ * seq, SEQ * (seq + 1))
             scores = lax.dot_general(q_buf[seq], k_buf[rows, :], (((1,), (1,)), ((), ())), preferred_element_type=F32) * HEAD_DIM ** -0.5
             scores = jnp.where(row >= col, scores, -jnp.inf)
@@ -328,25 +330,25 @@
         return SEQ // 2 * n, SEQ // 2
 
     def ag_start(l):
-        for n in range(2):
+        for n in BOTH:
             go(ag(l, n, 0, 2 + 2 * n))
         go(ag(l, 2, 0, 1))
 
     def ag_turn(l):
-        for n in range(2):
+        for n in BOTH:
             k = 2 + 2 * n
             ag(l, n, k, k).wait_recv()
             go(ag(l, 5 + n, k, 6 - k, *ag_half(n)))
             go(ag(l, 3 + n, k, 1))
 
     def ag_across(l):
-        for n in range(2):
+        for n in BOTH:
             ag(l, 5 + n, 6, 4 - 2 * n, *ag_half(n)).wait_recv()
             go(ag(l, 7 + n, 6, 1, *ag_half(n)))
 
     def ag_end(l):
         ag(l, 2, 1, 1).wait_recv()
-        for n in range(2):
+        for n in BOTH:
             ag(l, 3 + n, 3 + 2 * n, 1).wait_recv()
             ag(l, 7 + n, 7, 1, *ag_half(n)).wait_recv()
 
@@ -384,7 +386,7 @@
 
         lax.fori_loop(3 * half, 3 * half + 3, cols, 0)
 
-    A, B = slice(0, DIM // 2), slice(DIM // 2, DIM)
+    A, B = slice(DIM // 2), slice(DIM // 2, DIM)
 
     def chip_rows(yy, xx):
         return pl.ds(aligned(SEQ * (2 * yy + xx), SEQ), SEQ)
@@ -447,29 +449,29 @@
         relay_gu(l, 1, THREE)
         ag_end(l)
         gate_up(l, 0, 1 - c)
-        relay_gu(l, 1, FOUR)
+        relay_gu(l, 1, FOUR[:1] + FIVE[:2])
         while sends:
             sends.pop().wait_send()
         finish_wd(l)
-        for half in range(2):
+        for half in BOTH:
             down(l, 0, 1 - c, half)
-        relay_gu(l, 1, FIVE)
-        for half in range(2):
+        relay_gu(l, 1, FOUR[1:] + FIVE[2:])
+        for half in BOTH:
             down(l, 0, c, half)
         await_gu(l, 1)
         gate_up(l, 1, 1 - c)
-        for half in range(2):
+        for half in BOTH:
             down(l, 1, 1 - c, half)
             send(rs_core(l, half))
 
     def mlp_own(l):
         gate_up(l, 1, c)
-        for half in range(2):
+        for half in BOTH:
             down(l, 1, c, half)
             cols = (A, B)[half]
             rs_core(l, half).wait_recv()
             part[c, :, cols] = part[c, :, cols] + r1[l, :, cols]
-            for t in range(2):
+            for t in BOTH:
                 send((rs_a, rs_b)[half](l, t))
 
     def rs_add(l, t):
@@ -484,7 +486,7 @@
             send(rs_b_last(l))
 
     def rs_middle(l):
-        for t in range(2):
+        for t in BOTH:
             rs_add(l, t)
 
     def rs_end(l, out):
@@ -494,13 +496,13 @@
         out[:, B] = (mid[:, B].astype(F32) + (part[c, chip_rows(y, x), B] + r3b[l])).astype(BF)
 
     gain_mine[...] = jnp.zeros_like(gain_mine)
-    gain_mine[0:LAYERS, 0:ROWS] = an_ref[...].astype(F32)
-    gain_mine[LAYERS : 2 * LAYERS, 0:ROWS] = mn_ref[...].astype(F32)
+    gain_mine[:LAYERS, :ROWS] = an_ref[...].astype(F32)
+    gain_mine[LAYERS : 2 * LAYERS, :ROWS] = mn_ref[...].astype(F32)
     gain_mine[...] = jnp.where(c == 1, pltpu.roll(gain_mine[...], ROWS, 1), gain_mine[...])
     for k in range(1, 8):
         go(gain_copy(k))
     send_gu(0, 0, ONE + TWO + THREE)
-    for m in range(2):
+    for m in BOTH:
         send_attn(0, m)
     gains[me] = gain_mine[...]
     res[...] = x_ref[...]
@@ -510,7 +512,7 @@
         gain_rows[:, 384 * p : 384 * (p + 1)] = gains[2 * p] + gains[2 * p + 1]
     start_layer(0)
     relay_gu(0, 0, ONE + TWO + THREE)
-    for m in range(2):
+    for m in BOTH:
         relay_attn(0, m)
     send_gu(0, 0, FOUR + FIVE + CORE)
     for l in range(LAYERS):
@@ -527,8 +529,8 @@
     relay_gu(1, 0, TWO)
     relay_attn(1, 0)
     rs_middle(0)
+    send_gu(1, 0, THREE)
     send_attn(1, 1)
-    send_gu(1, 0, THREE)
     relay_attn_across(1, 0)
     rs_end(0, res)
     start_layer(1)
@@ -538,9 +540,9 @@
     relay_gu(1, 0, THREE)
     relay_attn_across(1, 1)
     attention_out(1)
-    relay_gu(1, 0, FOUR)
+    relay_gu(1, 0, FOUR[:1])
     attention_end(1)
-    mlp(1, FIVE)
+    mlp(1, FIVE[:1] + FOUR[1:] + FIVE[1:])
     mlp_own(1)
     rs_middle(1)
     rs_end(1, y_ref)
@@ -552,7 +554,7 @@
     vmem = pl.BlockSpec(memory_space=pltpu.VMEM)
     hbm = pl.BlockSpec(memory_space=pl.ANY)
     dma = pltpu.SemaphoreType.DMA
-    pairs = [(7,), (LAYERS, 3, 2), (LAYERS, 3, 2), (LAYERS, 3, 5), (LAYERS, 3), (LAYERS, 2, 2, 7), (LAYERS, 2, 2, 6), (LAYERS,), (LAYERS, 9), (LAYERS, 8)]
+    pairs = [(7,), (LAYERS, 4, 2), (LAYERS, 4, 2), (LAYERS, 4, 5), (LAYERS, 3), (LAYERS, 2, 2, 7), (LAYERS, 2, 2, 6), (LAYERS,), (LAYERS, 9), (LAYERS, 8)]
     inv_freq = ROPE_THETA ** -(np.arange(HEAD_DIM // 2) * 2.0 / HEAD_DIM)
     angles = np.tile(np.arange(SEQ)[:, None] * inv_freq[None, :].astype(np.float32), (2, 1)).astype(np.float32)
     cos_table = np.concatenate([np.cos(angles), np.cos(angles)], axis=1)
@@ -560,11 +562,11 @@
 
     def local_forward(hidden, attn_norm, w_q, w_k, w_v, w_o, mlp_norm, w_gate, w_up, w_down):
         wq = w_q.transpose(0, 2, 1, 3)
-        wkv = jnp.stack([w_k, w_v], axis=3).reshape(LAYERS, ROWS, 2 * KV_HEADS, HEAD_DIM).transpose(0, 2, 1, 3)
+        wk, wv = w_k.transpose(0, 2, 1, 3), w_v.transpose(0, 2, 1, 3)
         y = pl.pallas_call(
             kernel,
             out_shape=jax.ShapeDtypeStruct((SEQ, DIM), BF),
-            in_specs=[vmem] * 5 + [hbm] * 6,
+            in_specs=[vmem] * 5 + [hbm] * 7,
             out_specs=vmem,
             scratch_shapes=[
                 pltpu.VMEM((8, 2 * ROWS), F32),
@@ -593,9 +595,9 @@
                 pltpu.VMEM((LAYERS, 2, SEQ, DIM // 2), F32),
                 pltpu.VMEM((LAYERS, SEQ, DIM // 2), F32),
                 pltpu.VMEM((LAYERS, SEQ, DIM // 2), F32),
-            ] + [dma(shape) for shape in pairs for end in range(2)] + [dma((LAYERS, 3))] * 3,
+            ] + [dma(shape) for shape in pairs for end in BOTH] + [dma((LAYERS, 4))] * 3,
             compiler_params=pltpu.CompilerParams(collective_id=0, has_side_effects=True, vmem_limit_bytes=67043328),
-        )(hidden.reshape(SEQ, DIM), attn_norm, mlp_norm, jnp.asarray(cos_table), jnp.asarray(sin_table), wq, w_o, wkv, w_gate, w_up, w_down)
+        )(hidden.reshape(SEQ, DIM), attn_norm, mlp_norm, jnp.asarray(cos_table), jnp.asarray(sin_table), wq, w_o, wk, wv, w_gate, w_up, w_down)
         return y.reshape(1, SEQ, DIM)
 
     batch_spec = P(("dp", "fsdp"), None, None)

time: 199 us -> 197 us (0.990)
  no operation moved by 1% of the time
where the time goes in v6:
time: 197 us
  Pallas kernels  193 us (98%)
  local copies, waits for them, and re-layouts  3.43 us (2%)
    pallas_call x1, Pallas kernels, local_forward(): pl.pallas_call(kernel, out_shape=jax.ShapeDtypeStruct((SEQ, DIM), BF), in...  193 us

profile of v6, /device:TPU:0, one launch (start us, length us, event | category | flops | bytes accessed | tf_op | source)
XLA Modules:
  0.0 196.7 jit_solution(12378518316102373884)
XLA Ops:
  0.0 1.8 copy_bitcast_fusion
  1.8 193.3 %shard_map.118 = bf16[64,1536]{1,0:T(8,128)(2,1)} custom-call(bf16[64,1536]{1,0:T(8,128)(2,1)} %bitcast.9, bf16[2,192]{1,0:T(2,128)(2,1)} %an_ref.1, bf16[2,192]{1,0:T(2,128)(2,1)} %mn_ref.1, f32[128,128]{1,0:T(8,128)} %constant.4.clone.cos_ref, f32[128,128]{1,0:T(8,128)} %constant.5.clone.sin_ref, bf16[2,12,192,128]{3,2,1,0:T(8,128)(2,1)} %bitcast.7, ...), custom_call_target="tpu_custom_call" | custom-call | tf_op jit(solution)/shard_map/pallas_call | solution.py:566
  195.1 1.6 copy.18

commit v7 on v6

--- a/solution.py
+++ b/solution.py
@@ -28,7 +28,7 @@
 MAIN = 1088
 EDGE = 32
 HALF = ROWS // 2
-DIRECT = ((96, 128), (96, 128))
+DIRECT = ((96, 96), (144, 96))
 BF = jnp.bfloat16
 BOTH = range(2)
 F32 = jnp.float32
@@ -170,21 +170,21 @@
         return wgu.at[l, g, pl.ds(aligned(ROWS * peer(k) + start, 16), count), pl.ds(*PARTS[p])]
 
     def gu_direct(l, p, g, k):
-        start, count = (0, ROWS) if k == 1 else (aligned((ROWS - DIRECT[l][p]) * z, 16), DIRECT[l][p])
+        start, count = (0, ROWS) if k == 1 else (aligned((ROWS - DIRECT[p][k // 6]) * z, 16), DIRECT[p][k // 6])
         src = halves[g].at[l, pl.ds(start, count), pl.ds(aligned(window(peer(k)) + PARTS[p][0], LANES), PARTS[p][1])]
         return remote(src, gu_rows(l, p, g, 0, start, count), gd_s.at[l, p, g, k - 1], gd_r.at[l, p, g, k - 1], plane(k))
 
     def gu_arrival(l, p, g, k):
-        start, count = (0, ROWS) if k == 1 else ((ROWS - DIRECT[l][p]) * z, DIRECT[l][p])
+        start, count = (0, ROWS) if k == 1 else ((ROWS - DIRECT[p][k // 6]) * z, DIRECT[p][k // 6])
         dst = gu_rows(l, p, g, k, start, count)
         return remote(dst, dst, gd_s.at[l, p, g, k - 1], gd_r.at[l, p, g, k - 1], plane(k))
 
     def gu_across(l, p, g, k):
-        rows = gu_rows(l, p, g, k, DIRECT[l][p] * z, ROWS - DIRECT[l][p])
+        rows = gu_rows(l, p, g, k, DIRECT[p][k // 6] * z, ROWS - DIRECT[p][k // 6])
         return remote(rows, rows, gz_s.at[l, p, g, k - 2], gz_r.at[l, p, g, k - 2], across)
 
     def gu_across_arrival(l, p, g, k):
-        dst = gu_rows(l, p, g, k, DIRECT[l][p] * (1 - z), ROWS - DIRECT[l][p])
+        dst = gu_rows(l, p, g, k, DIRECT[p][k // 6] * (1 - z), ROWS - DIRECT[p][k // 6])
         return remote(dst, dst, gz_s.at[l, p, g, k - 2], gz_r.at[l, p, g, k - 2], across)
 
     def gu_own(l, g):

time: 197 us -> 196 us (level)
  no operation moved by 1% of the time
where the time goes in v7:
time: 196 us
  Pallas kernels  193 us (98%)
  local copies, waits for them, and re-layouts  3.43 us (2%)
    pallas_call x1, Pallas kernels, local_forward(): pl.pallas_call(kernel, out_shape=jax.ShapeDtypeStruct((SEQ, DIM), BF), in...  193 us

profile of v7, /device:TPU:0, one launch (start us, length us, event | category | flops | bytes accessed | tf_op | source)
XLA Modules:
  0.0 196.2 jit_solution(1054084570439260081)
XLA Ops:
  0.0 1.8 copy_bitcast_fusion
  1.8 192.8 %shard_map.118 = bf16[64,1536]{1,0:T(8,128)(2,1)} custom-call(bf16[64,1536]{1,0:T(8,128)(2,1)} %bitcast.9, bf16[2,192]{1,0:T(2,128)(2,1)} %an_ref.1, bf16[2,192]{1,0:T(2,128)(2,1)} %mn_ref.1, f32[128,128]{1,0:T(8,128)} %constant.4.clone.cos_ref, f32[128,128]{1,0:T(8,128)} %constant.5.clone.sin_ref, bf16[2,12,192,128]{3,2,1,0:T(8,128)(2,1)} %bitcast.7, ...), custom_call_target="tpu_custom_call" | custom-call | tf_op jit(solution)/shard_map/pallas_call | solution.py:566
  194.6 1.6 copy.18

commit v8 on v7

--- a/solution.py
+++ b/solution.py
@@ -370,9 +370,10 @@
             columns(begin + TILE * n, TILE)
             return carry
 
-        lax.fori_loop(0, size // TILE, cols, 0)
-        if size % TILE:
-            columns(begin + size - LANES, LANES)
+        if p == 1:
+            columns(begin, size)
+        else:
+            lax.fori_loop(0, size // TILE, cols, 0)
 
     def down(l, p, b, half):
         rows = pl.ds(aligned(TILE * b, TILE), TILE)
@@ -384,7 +385,7 @@
             part[b, :, at] = add if p == 0 else part[b, :, at] + add
             return carry
 
-        lax.fori_loop(3 * half, 3 * half + 3, cols, 0)
+        lax.fori_loop(3 * half, 3 * half + 3, cols, 0, unroll=p == 1)
 
     A, B = slice(DIM // 2), slice(DIM // 2, DIM)
 

time: 196 us -> 195 us (level)
  no operation moved by 1% of the time
where the time goes in v8:
time: 195 us
  Pallas kernels  192 us (98%)
  local copies, waits for them, and re-layouts  3.43 us (2%)
    pallas_call x1, Pallas kernels, local_forward(): pl.pallas_call(kernel, out_shape=jax.ShapeDtypeStruct((SEQ, DIM), BF), in...  192 us

profile of v8, /device:TPU:0, one launch (start us, length us, event | category | flops | bytes accessed | tf_op | source)
XLA Modules:
  0.0 195.3 jit_solution(7877167284001182806)
XLA Ops:
  0.0 1.8 copy_bitcast_fusion
  1.8 191.8 %shard_map.118 = bf16[64,1536]{1,0:T(8,128)(2,1)} custom-call(bf16[64,1536]{1,0:T(8,128)(2,1)} %bitcast.9, bf16[2,192]{1,0:T(2,128)(2,1)} %an_ref.1, bf16[2,192]{1,0:T(2,128)(2,1)} %mn_ref.1, f32[128,128]{1,0:T(8,128)} %constant.4.clone.cos_ref, f32[128,128]{1,0:T(8,128)} %constant.5.clone.sin_ref, bf16[2,12,192,128]{3,2,1,0:T(8,128)(2,1)} %bitcast.7, ...), custom_call_target="tpu_custom_call" | custom-call | tf_op jit(solution)/shard_map/pallas_call | solution.py:567
  193.7 1.6 copy.18
